TPU v7x, 16 devices: a 4x2x1 block of a 4x4x8 slice. The times are simulated.
16 devices in a mesh: dp: 2 (over y, z), tp: 8 (over x, core).
Axes of the slice: x: 4, y: 2, z: 1, core: 2. Of those that a mesh axis runs over, the one named last changes fastest.
The devices are a block of a 4x4x8 slice.
Arguments:
- y_one: float32 [16, 32, 2048], P('dp'), parts along dimension 0
- y_two: float32 [16, 32, 2048], P('dp'), parts along dimension 0
- dy_one: float32 [16, 32, 2048], P('dp'), parts along dimension 0
- dy_two: float32 [16, 32, 2048], P('dp'), parts along dimension 0
- seq_lens: int32 [16], P('dp'), parts along dimension 0
- w_query: bfloat16 [4, 2048, 32, 64], P(None, None, 'tp')
- w_key: bfloat16 [4, 2048, 8, 64], P(None, None, 'tp')
- w_value: bfloat16 [4, 2048, 8, 64], P(None, None, 'tp')
- w_out: bfloat16 [4, 32, 64, 2048], P(None, 'tp')
- w_up: bfloat16 [4, 2048, 5632], P(None, None, 'tp')
- w_down: bfloat16 [4, 5632, 2048], P(None, 'tp')
Outputs:
- output 1: float32 [16, 32, 2048], P('dp'), parts along dimension 0
- output 2: float32 [16, 32, 2048], P('dp'), parts along dimension 0
- output 3: float32 [16, 32, 2048], P('dp'), parts along dimension 0
- output 4: float32 [16, 32, 2048], P('dp'), parts along dimension 0
- output 5: float32 [8, 2048, 32, 64], P('dp', None, 'tp'), parts along dimension 0
- output 6: float32 [8, 2048, 8, 64], P('dp', None, 'tp'), parts along dimension 0
- output 7: float32 [8, 2048, 8, 64], P('dp', None, 'tp'), parts along dimension 0
- output 8: float32 [8, 32, 64, 2048], P('dp', 'tp'), parts along dimension 0
- output 9: float32 [8, 2048, 5632], P('dp', None, 'tp'), parts along dimension 0
- output 10: float32 [8, 5632, 2048], P('dp', 'tp'), parts along dimension 0
There are 2 independent parts. A program takes and returns all parts, laid end to end along the dimension named above; an argument that names none is the same for every part.
All inputs are finite; a program needn't handle non-finite values.
Results may differ from a plain program's by a relative error of at most 0.02.
Values are sent between devices in bfloat16 or wider.
A program may use at most 768 MiB of HBM per device.

v0:
```python
import jax
import jax.numpy as jnp
from jax import lax
from jax.sharding import PartitionSpec as P, NamedSharding

F32 = jnp.float32
BF16 = jnp.bfloat16
EPS = 1e-5
MASK_VALUE = -1e30


def rms_norm(x_val):
    inv_rms = lax.rsqrt(jnp.mean(x_val * x_val, axis=-1, keepdims=True) + EPS)
    return x_val * inv_rms, inv_rms


def rms_back(normed, inv_rms, grad_norm):
    return inv_rms * (grad_norm - normed * jnp.mean(grad_norm * normed, axis=-1, keepdims=True))


def visible_mask(seq_lens, seq_len):
    row_pos = lax.broadcasted_iota(jnp.int32, (seq_len, seq_len), 0)
    col_pos = lax.broadcasted_iota(jnp.int32, (seq_len, seq_len), 1)
    causal = (col_pos <= row_pos)[None, None, None]
    in_length = col_pos[None, None, None] < seq_lens[:, None, None, None, None]
    return causal & in_length


def block_back(carry, seq_lens, layer_w, all_reduce):
    y_one, y_two, dy_one, dy_two = carry
    w_query, w_key, w_value, w_out, w_up, w_down = layer_w
    n_batch, seq_len = y_one.shape[0], y_one.shape[1]
    n_heads, head_dim = w_query.shape[1], w_query.shape[2]
    kv_slots = w_key.shape[1]
    group_size = n_heads // kv_slots
    score_scale = head_dim ** -0.5

    norm_g, inv_g = rms_norm(y_one)
    norm_g_b = norm_g.astype(BF16)
    pre_act = jnp.einsum('bsd,df->bsf', norm_g_b, w_up, preferred_element_type=F32)
    act_val, gelu_back = jax.vjp(jax.nn.gelu, pre_act)
    act_b = act_val.astype(BF16)
    x_two = y_two - all_reduce(jnp.einsum('bsf,fd->bsd', act_b, w_down, preferred_element_type=F32))
    dy2_b = dy_two.astype(BF16)
    d_act = jnp.einsum('bsd,fd->bsf', dy2_b, w_down, preferred_element_type=F32)
    d_pre = gelu_back(d_act)[0].astype(BF16)
    dw_down = jnp.einsum('bsf,bsd->fd', act_b, dy2_b, preferred_element_type=F32)
    dw_up = jnp.einsum('bsd,bsf->df', norm_g_b, d_pre, preferred_element_type=F32)
    grad_norm_g = all_reduce(jnp.einsum('bsf,df->bsd', d_pre, w_up, preferred_element_type=F32))
    dy_one = dy_one + rms_back(norm_g, inv_g, grad_norm_g)

    norm_f, inv_f = rms_norm(x_two)
    norm_f_b = norm_f.astype(BF16)
    query_proj = jnp.einsum('bsd,dhe->bshe', norm_f_b, w_query, preferred_element_type=F32).astype(BF16)
    query_grp = query_proj.reshape(n_batch, seq_len, kv_slots, group_size, head_dim)
    key_proj = jnp.einsum('bsd,dge->bsge', norm_f_b, w_key, preferred_element_type=F32).astype(BF16)
    value_proj = jnp.einsum('bsd,dge->bsge', norm_f_b, w_value, preferred_element_type=F32).astype(BF16)
    scores = jnp.einsum('bigre,bjge->bgrij', query_grp, key_proj, preferred_element_type=F32) * score_scale
    scores = jnp.where(visible_mask(seq_lens, seq_len), scores, MASK_VALUE)
    attn_probs = jax.nn.softmax(scores, axis=-1)
    probs_b = attn_probs.astype(BF16)
    attn_out = jnp.einsum('bgrij,bjge->bigre', probs_b, value_proj, preferred_element_type=F32).astype(BF16)
    attn_out = attn_out.reshape(n_batch, seq_len, n_heads, head_dim)
    x_one = y_one - all_reduce(jnp.einsum('bihe,hed->bid', attn_out, w_out, preferred_element_type=F32))
    dy1_b = dy_one.astype(BF16)
    dw_out = jnp.einsum('bihe,bid->hed', attn_out, dy1_b, preferred_element_type=F32)
    d_attn = jnp.einsum('bid,hed->bihe', dy1_b, w_out, preferred_element_type=F32).astype(BF16)
    d_attn = d_attn.reshape(n_batch, seq_len, kv_slots, group_size, head_dim)
    d_value = jnp.einsum('bgrij,bigre->bjge', probs_b, d_attn, preferred_element_type=F32).astype(BF16)
    d_probs = jnp.einsum('bigre,bjge->bgrij', d_attn, value_proj, preferred_element_type=F32)
    d_scores = (attn_probs * (d_probs - jnp.sum(d_probs * attn_probs, axis=-1, keepdims=True)) * score_scale).astype(BF16)
    d_query = jnp.einsum('bgrij,bjge->bigre', d_scores, key_proj, preferred_element_type=F32).astype(BF16)
    d_query = d_query.reshape(n_batch, seq_len, n_heads, head_dim)
    d_key = jnp.einsum('bgrij,bigre->bjge', d_scores, query_grp, preferred_element_type=F32).astype(BF16)
    dw_query = jnp.einsum('bsd,bshe->dhe', norm_f_b, d_query, preferred_element_type=F32)
    dw_key = jnp.einsum('bsd,bsge->dge', norm_f_b, d_key, preferred_element_type=F32)
    dw_value = jnp.einsum('bsd,bsge->dge', norm_f_b, d_value, preferred_element_type=F32)
    grad_norm_f = all_reduce(jnp.einsum('bshe,dhe->bsd', d_query, w_query, preferred_element_type=F32)
                             + jnp.einsum('bsge,dge->bsd', d_key, w_key, preferred_element_type=F32)
                             + jnp.einsum('bsge,dge->bsd', d_value, w_value, preferred_element_type=F32))
    dx_two = dy_two + rms_back(norm_f, inv_f, grad_norm_f)
    return (x_one, x_two, dy_one, dx_two), (dw_query, dw_key, dw_value, dw_out, dw_up, dw_down)


def stack_grads(grads_by_layer):
    return tuple(jnp.stack([layer_grads[grad_pos] for layer_grads in grads_by_layer]) for grad_pos in range(6))


def tp_sum(partial_val):
    return lax.psum(partial_val, 'tp')


def solution(mesh):
    act_spec = P('dp', None, None)
    w_specs = (P(None, None, 'tp', None), P(None, None, 'tp', None), P(None, None, 'tp', None),
               P(None, 'tp', None, None), P(None, None, 'tp'), P(None, 'tp', None))
    g_specs = (P('dp', None, 'tp', None), P('dp', None, 'tp', None), P('dp', None, 'tp', None),
               P('dp', 'tp', None, None), P('dp', None, 'tp'), P('dp', 'tp', None))

    def local_fn(y_one, y_two, dy_one, dy_two, seq_lens, w_query, w_key, w_value, w_out, w_up, w_down):
        weights = (w_query, w_key, w_value, w_out, w_up, w_down)
        carry = (y_one, y_two, dy_one, dy_two)
        n_layers = w_query.shape[0]
        grads_by_layer = [None] * n_layers
        for layer_idx in reversed(range(n_layers)):
            layer_w = tuple(w_stack[layer_idx] for w_stack in weights)
            carry, grads_by_layer[layer_idx] = block_back(carry, seq_lens, layer_w, tp_sum)
        return carry + stack_grads(grads_by_layer)

    return jax.shard_map(local_fn, mesh=mesh,
                         in_specs=(act_spec,) * 4 + (P('dp'),) + w_specs,
                         out_specs=(act_spec,) * 4 + g_specs,
                         check_vma=False)
```

profile of v0, /device:TPU:113, one launch (start us, length us, event | category | flops | bytes accessed | tf_op | source)
XLA Modules:
  0.0 695.1 jit_solution(12556506162349873261)
XLA Ops:
  12.3 4.5 fusion.26
  16.8 3.2 fusion.142
  20.8 4.1 fusion.28
  25.7 64.7 %all-reduce.31.cloned.1.call-done = (f32[8,32,2048]{2,1,0:T(8,128)}, f32[8,32,2048]{2,1,0:T(8,128)}) async-done(((f32[8,32,2048]{2,1,0:T(8,128)}, f32[8,32,2048]{2,1,0:T(8,128)}), (f32[8,32,2048]{2,1,0:T(8,128)}, f32[8,32,2048]{2,1,0:T(8,128)})) %all-reduce.31.cloned.1.call-update) | async-done | bytes 4194320 | tf_op jit(solution)/shard_map/psum | solution.py:90
  108.4 63.9 %all-reduce.29.cloned.1.call-done = (f32[8,32,2048]{2,1,0:T(8,128)}, f32[8,32,2048]{2,1,0:T(8,128)}) async-done(((f32[8,32,2048]{2,1,0:T(8,128)}, f32[8,32,2048]{2,1,0:T(8,128)}), (f32[8,32,2048]{2,1,0:T(8,128)}, f32[8,32,2048]{2,1,0:T(8,128)})) %all-reduce.29.cloned.1.call-update) | async-done | bytes 4194320 | tf_op jit(solution)/shard_map/psum | solution.py:90
  181.4 4.5 fusion.18
  185.9 3.2 fusion.149
  189.9 4.1 fusion.20
  194.2 64.2 %all-reduce.27.cloned.1.call-done = (f32[8,32,2048]{2,1,0:T(8,128)}, f32[8,32,2048]{2,1,0:T(8,128)}) async-done(((f32[8,32,2048]{2,1,0:T(8,128)}, f32[8,32,2048]{2,1,0:T(8,128)}), (f32[8,32,2048]{2,1,0:T(8,128)}, f32[8,32,2048]{2,1,0:T(8,128)})) %all-reduce.27.cloned.1.call-update) | async-done | bytes 4194320 | tf_op jit(solution)/shard_map/psum | solution.py:90
  277.4 5.3 convolution_bitcast_fusion.4
  282.7 3.6 convolution_bitcast_fusion
  292.4 48.7 %all-reduce.25.cloned.1.call-done = (f32[8,32,2048]{2,1,0:T(8,128)}, f32[8,32,2048]{2,1,0:T(8,128)}) async-done(((f32[8,32,2048]{2,1,0:T(8,128)}, f32[8,32,2048]{2,1,0:T(8,128)}), (f32[8,32,2048]{2,1,0:T(8,128)}, f32[8,32,2048]{2,1,0:T(8,128)})) %all-reduce.25.cloned.1.call-update) | async-done | bytes 4194320 | tf_op jit(solution)/shard_map/psum | solution.py:90
  347.1 4.0 fusion.14
  351.2 4.5 fusion.10
  355.7 3.2 fusion.156
  358.9 4.3 fusion.12
  364.1 3.5 convolution_bitcast_fusion.5
  367.7 3.5 convolution_bitcast_fusion.1
  377.3 50.2 %all-reduce.23.cloned.1.call-done = (f32[8,32,2048]{2,1,0:T(8,128)}, f32[8,32,2048]{2,1,0:T(8,128)}) async-done(((f32[8,32,2048]{2,1,0:T(8,128)}, f32[8,32,2048]{2,1,0:T(8,128)}), (f32[8,32,2048]{2,1,0:T(8,128)}, f32[8,32,2048]{2,1,0:T(8,128)})) %all-reduce.23.cloned.1.call-update) | async-done | bytes 4194320 | tf_op jit(solution)/shard_map/psum | solution.py:90
  445.5 4.7 convolution_bitcast_fusion.6
  450.2 3.5 convolution_bitcast_fusion.2
  459.9 49.6 %all-reduce.21.cloned.1.call-done = (f32[8,32,2048]{2,1,0:T(8,128)}, f32[8,32,2048]{2,1,0:T(8,128)}) async-done(((f32[8,32,2048]{2,1,0:T(8,128)}, f32[8,32,2048]{2,1,0:T(8,128)}), (f32[8,32,2048]{2,1,0:T(8,128)}, f32[8,32,2048]{2,1,0:T(8,128)})) %all-reduce.21.cloned.1.call-update) | async-done | bytes 4194320 | tf_op jit(solution)/shard_map/psum | solution.py:90
  518.6 4.0 convolution_bitcast_fusion.3
  527.6 4.1 fusion.4
  533.2 19.0 %pad_maximum_fusion.1 = f32[4,704,2048]{2,1,0:T(8,128)} fusion(f32[1,704,2048]{2,1,0:T(8,128)} %convolution_bitcast_fusion, f32[1,704,2048]{2,1,0:T(8,128)} %convolution_bitcast_fusion.1, f32[1,704,2048]{2,1,0:T(8,128)} %convolution_bitcast_fusion.2, f32[1,704,2048]{2,1,0:T(8,128)} %convolution_bitcast_fusion.3), kind=kLoop, calls=%fused_computation.1 | loop fusion | flops 17301504 | bytes 46137344 | tf_op jit(solution)/shard_map/stack | solution.py:86
  552.2 8.4 %pad_maximum_fusion = f32[4,2048,704]{1,2,0:T(8,128)} fusion(f32[1,2048,704]{1,2,0:T(8,128)S(1)} %bitcast.689, f32[1,2048,704]{1,2,0:T(8,128)S(1)} %bitcast.691, f32[1,2048,704]{1,2,0:T(8,128)S(1)} %bitcast.693, f32[1,2048,704]{1,2,0:T(8,128)S(1)} %convolution_bitcast_fusion.7), kind=kLoop, calls=%fused_computation | loop fusion | flops 17301504 | bytes 46137344 | tf_op jit(solution)/shard_map/stack | solution.py:86
  560.6 35.4 %all-reduce.19.cloned.1.call-done = (f32[8,32,2048]{2,1,0:T(8,128)}, f32[8,32,2048]{2,1,0:T(8,128)}) async-done(((f32[8,32,2048]{2,1,0:T(8,128)}, f32[8,32,2048]{2,1,0:T(8,128)}), (f32[8,32,2048]{2,1,0:T(8,128)}, f32[8,32,2048]{2,1,0:T(8,128)})) %all-reduce.19.cloned.1.call-update) | async-done | bytes 4194320 | tf_op jit(solution)/shard_map/psum | solution.py:90
  615.4 3.2 pad_maximum_fusion.5
  623.9 4.4 pad_maximum_fusion.3
  629.7 3.7 pad_maximum_fusion.2
  633.3 45.9 %all-reduce.17.cloned.1.call-done = (f32[8,32,2048]{2,1,0:T(8,128)}, f32[8,32,2048]{2,1,0:T(8,128)}) async-done(((f32[8,32,2048]{2,1,0:T(8,128)}, f32[8,32,2048]{2,1,0:T(8,128)}), (f32[8,32,2048]{2,1,0:T(8,128)}, f32[8,32,2048]{2,1,0:T(8,128)})) %all-reduce.17.cloned.1.call-update) | async-done | bytes 4194320 | tf_op jit(solution)/shard_map/psum | solution.py:90
  682.7 3.5 multiply_add_fusion
  (376 shorter events, 142.7 us)
Async XLA Ops:
  7.2 83.2 %all-reduce.31.cloned.1.call-start = ((), (), s32[]{:S(2)}) async-start(), calls=%async_computation.7 | async-start | bytes 8388608 | tf_op jit(solution)/shard_map/psum | solution.py:90
  12.3 4.6 copy-start.97
  25.0 147.4 %all-reduce.29.cloned.1.call-start = ((), (), s32[]{:S(2)}) async-start(), calls=%async_computation.6 | async-start | bytes 8388608 | tf_op jit(solution)/shard_map/psum | solution.py:90
  108.1 64.3 %copy-start.11 = (f32[8,32,2048]{2,1,0:T(8,128)S(1)}, f32[8,32,2048]{2,1,0:T(8,128)}, u32[]{:S(2)}) copy-start(f32[8,32,2048]{2,1,0:T(8,128)} %copy-done.10) | copy-start | bytes 6291460
  108.1 150.2 %all-reduce.27.cloned.1.call-start = ((), (), s32[]{:S(2)}) async-start(), calls=%async_computation.5 | async-start | bytes 8388608 | tf_op jit(solution)/shard_map/psum | solution.py:90
  175.7 10.3 %copy-start.25 = (f32[8,32,2048]{2,1,0:T(8,128)}, f32[8,32,2048]{2,1,0:T(8,128)S(1)}, u32[]{:S(2)}) copy-start(f32[8,32,2048]{2,1,0:T(8,128)S(1)} %multiply_add_fusion.6) | copy-start | bytes 6291460
  181.4 4.6 copy-start.99
  194.1 147.0 %all-reduce.25.cloned.1.call-start = ((), (), s32[]{:S(2)}) async-start(), calls=%async_computation.4 | async-start | bytes 8388608 | tf_op jit(solution)/shard_map/psum | solution.py:90
  276.9 150.6 %all-reduce.23.cloned.1.call-start = ((), (), s32[]{:S(2)}) async-start(), calls=%async_computation.3 | async-start | bytes 8388608 | tf_op jit(solution)/shard_map/psum | solution.py:90
  277.4 5.3 copy-start.59
  277.4 5.3 copy-start.98
  346.8 8.9 %copy-start.30 = (f32[8,32,2048]{2,1,0:T(8,128)}, f32[8,32,2048]{2,1,0:T(8,128)S(1)}, u32[]{:S(2)}) copy-start(f32[8,32,2048]{2,1,0:T(8,128)S(1)} %multiply_add_fusion.4) | copy-start | bytes 6291460
  363.2 146.2 %all-reduce.21.cloned.1.call-start = ((), (), s32[]{:S(2)}) async-start(), calls=%async_computation.2 | async-start | bytes 8388608 | tf_op jit(solution)/shard_map/psum | solution.py:90
  367.7 4.7 copy-start.85
  375.6 52.0 %copy-start.7 = (f32[8,32,2048]{2,1,0:T(8,128)S(1)}, f32[8,32,2048]{2,1,0:T(8,128)}, u32[]{:S(2)}) copy-start(f32[8,32,2048]{2,1,0:T(8,128)} %copy-done.5) | copy-start | bytes 6291460
  445.2 150.8 %all-reduce.19.cloned.1.call-start = ((), (), s32[]{:S(2)}) async-start(), calls=%async_computation.1 | async-start | bytes 8388608 | tf_op jit(solution)/shard_map/psum | solution.py:90
  445.5 4.7 copy-start.31
  445.5 4.7 copy-start.102
  458.0 51.4 %copy-start.9 = (f32[8,32,2048]{2,1,0:T(8,128)S(1)}, f32[8,32,2048]{2,1,0:T(8,128)}, u32[]{:S(2)}) copy-start(f32[8,32,2048]{2,1,0:T(8,128)} %copy-done.8) | copy-start | bytes 6291460
  512.8 9.9 %copy-start.28 = (f32[8,32,2048]{2,1,0:T(8,128)}, f32[8,32,2048]{2,1,0:T(8,128)S(1)}, u32[]{:S(2)}) copy-start(f32[8,32,2048]{2,1,0:T(8,128)S(1)} %multiply_add_fusion.2) | copy-start | bytes 6291460
  515.6 7.0 %slice-start.6 = ((s8[11534336]{0:T(1024)(128)(4,1)}), s8[4194304]{0:T(1024)(128)(4,1)S(1)}, s32[]{:S(2)}) async-start(s8[11534336]{0:T(1024)(128)(4,1)} %bitcast.694), calls=%async_computation.14 | async-start | bytes 8388608
  518.6 5.2 slice-start.8
  531.8 147.5 %all-reduce.17.cloned.1.call-start = ((), (), s32[]{:S(2)}) async-start(), calls=%async_computation | async-start | bytes 8388608 | tf_op jit(solution)/shard_map/psum | solution.py:90
  532.1 20.1 %slice-start = ((s8[5767168]{0:T(1024)(128)(4,1)}), s8[4194304]{0:T(1024)(128)(4,1)S(1)}, s32[]{:S(2)}) async-start(s8[5767168]{0:T(1024)(128)(4,1)} %bitcast.688), calls=%async_computation.8 | async-start | bytes 8388608
  532.1 20.1 %slice-start.2 = ((s8[5767168]{0:T(1024)(128)(4,1)}), s8[4194304]{0:T(1024)(128)(4,1)S(1)}, s32[]{:S(2)}) async-start(s8[5767168]{0:T(1024)(128)(4,1)} %bitcast.690), calls=%async_computation.10 | async-start | bytes 8388608
  532.1 20.1 %slice-start.4 = ((s8[5767168]{0:T(1024)(128)(4,1)}), s8[4194304]{0:T(1024)(128)(4,1)S(1)}, s32[]{:S(2)}) async-start(s8[5767168]{0:T(1024)(128)(4,1)} %bitcast.692), calls=%async_computation.12 | async-start | bytes 8388608
  533.1 19.1 %slice-start.1 = ((s8[5767168]{0:T(1024)(128)(4,1)}), s8[1572864]{0:T(1024)(128)(4,1)S(1)}, s32[]{:S(2)}) async-start(s8[5767168]{0:T(1024)(128)(4,1)} %bitcast.688), calls=%async_computation.9 | async-start | bytes 3145728
  533.1 19.1 %slice-start.3 = ((s8[5767168]{0:T(1024)(128)(4,1)}), s8[1572864]{0:T(1024)(128)(4,1)S(1)}, s32[]{:S(2)}) async-start(s8[5767168]{0:T(1024)(128)(4,1)} %bitcast.690), calls=%async_computation.11 | async-start | bytes 3145728
  533.2 19.1 %slice-start.5 = ((s8[5767168]{0:T(1024)(128)(4,1)}), s8[1572864]{0:T(1024)(128)(4,1)S(1)}, s32[]{:S(2)}) async-start(s8[5767168]{0:T(1024)(128)(4,1)} %bitcast.692), calls=%async_computation.13 | async-start | bytes 3145728
  607.9 5.3 copy-start.80
  623.9 4.6 copy-start.45
  623.9 5.8 copy-start.46
  (88 other events, 216.4 us)
Sparse Core Ops, SparseCore 0:
  25.1 65.2 all-reduce.30
  108.3 64.0 all-reduce.28
  194.2 64.0 all-reduce.26
  277.0 64.0 all-reduce.24
  363.3 64.1 all-reduce.22
  445.4 64.0 all-reduce.20
  531.9 64.0 all-reduce.18
  615.2 64.0 all-reduce.16
where the time goes:
time: 706 us; the launch traced here: 695 us
  waiting for transfers between devices  423 us (60%)
  matrix products  141 us (20%)
  other arithmetic  77.6 us (11%)
  local copies, waits for them, and re-layouts  36 us (5%)
  between operations  15.7 us (2%)
    psum x8, waiting for transfers between devices, tp_sum(): return lax.psum(partial_val, 'tp')  423 us
    another operation x6, other arithmetic, stack_grads(): jnp.stack([layer_grads[grad_pos] for layer_grads in grads_by_layer])  40.1 us
    unnamed x224, local copies, waits for them, and re-layouts  36 us
    dot_general x4, matrix products, block_back(): jnp.einsum('bsf,df->bsd', d_pre, w_up, preferred_element_type=F32)  16.7 us
    dot_general x4, matrix products, block_back(): jnp.einsum('bsf,fd->bsd', act_b, w_down, preferred_element_type=F32)  16 us
    dot_general x4, matrix products, block_back(): jnp.einsum('bsf,bsd->fd', act_b, dy2_b, preferred_element_type=F32)  14.6 us
    dot_general x4, matrix products, block_back(): jnp.einsum('bsd,bsf->df', norm_g_b, d_pre, preferred_element_type=F32)  14.5 us
  transfers between devices with their start and end apart: 8, of which 8 were waited for; matrix products, arithmetic and copies ran while one was open for 12% of the time, Pallas kernels for 0%

commit v1 on v0

v1 whole, which is shorter than its diff:
```python
import functools

import jax
import jax.numpy as jnp
from jax import lax
from jax.experimental import pallas as pl
from jax.experimental.pallas import tpu as pltpu
from jax.sharding import PartitionSpec as P

F32 = jnp.float32
BF16 = jnp.bfloat16
EPS = 1e-5
MASK_VALUE = -1e30
GELU_C = 0.7978845608028654
GELU_A = 0.044715
MESH = pl.DeviceIdType.MESH
NT = (((1,), (1,)), ((), ()))
NN = (((1,), (0,)), ((), ()))
TN = (((0,), (0,)), ((), ()))


def mm(lhs, rhs, dims):
    return lax.dot_general(lhs, rhs, dims, preferred_element_type=F32)


def chain_kernel(cfg, lens, y1_h, y2_h, dy1_h, dy2_h, w1_h, w2_h, wq_h, wk_h, wv_h, wo_h,
                 fin_h, n1_o, n2_o, c_o, e_o, h_o, u_o, a_o, d_o,
                 n1, n2, cc, ee, w1, w2, wqkv, wo, h_s, u_s, gp, qkv, att, dqkv, probs, mask,
                 x1, x2, dy1, dy2, part, ra, rb, rc,
                 w_sem, in_sem, out_sem, fin_sem, rs_send, rs_recv, ag_send, ag_recv):
    n_layers, tp, seq, width, heads, hd = cfg
    chips = tp // 2
    tokens = tp * seq
    half = seq // 2
    scale = hd ** -0.5
    qw = heads * hd
    me = lax.axis_index('tp')
    chip = me // 2
    core = me - 2 * chip
    partner = me + 1 - 2 * core
    right = lax.rem(me + 2, tp)
    left = lax.rem(me + tp - 2, tp)
    opp = lax.rem(me + chips, tp)

    def rows(start, size=seq):
        return pl.ds(pl.multiple_of(start, half), size)

    def blk(ref, who):
        return ref.at[rows(who * seq)]

    def blk_a(ref, who):
        return ref.at[rows(who * seq, half)]

    def blk_b(ref, who):
        return ref.at[rows(who * seq + half, half)]

    def rcopy(src, dst, send, recv, dev):
        return pltpu.make_async_remote_copy(src_ref=src, dst_ref=dst, send_sem=send, recv_sem=recv,
                                            device_id={'tp': dev}, device_id_type=MESH)

    def w_copies(step):
        layer = n_layers - 1 - step
        slot = lax.rem(step, 2)
        kw = wk_h.shape[1]
        return (pltpu.make_async_copy(w1_h.at[layer], w1.at[slot], w_sem.at[slot, 0]),
                pltpu.make_async_copy(w2_h.at[layer], w2.at[slot], w_sem.at[slot, 1]),
                pltpu.make_async_copy(wq_h.at[layer], wqkv.at[slot, pl.ds(0, qw)], w_sem.at[slot, 2]),
                pltpu.make_async_copy(wk_h.at[layer], wqkv.at[slot, pl.ds(qw, kw)], w_sem.at[slot, 3]),
                pltpu.make_async_copy(wv_h.at[layer], wqkv.at[slot, pl.ds(qw + kw, kw)], w_sem.at[slot, 4]),
                pltpu.make_async_copy(wo_h.at[layer], wo.at[slot], w_sem.at[slot, 5]))

    owners = (opp, right, left, me)

    def rs_d2d(i, role):
        own = owners[role]
        theirs = own + 1 - 2 * core
        return rcopy(blk(part.at[i], theirs), ra.at[i, role], rs_send.at[i, role], rs_recv.at[i, role], partner)

    def rs_ring(i, kind):
        pt = part.at[i]
        lo, hi = pl.ds(0, half), pl.ds(half, half)
        src, dst, dev = ((blk_a(pt, opp), rb.at[i, 0], right), (blk_b(pt, opp), rb.at[i, 1], left),
                         (blk_b(pt, right), rc.at[i, 0, hi], right), (blk_a(pt, left), rc.at[i, 1, lo], left),
                         (blk_a(pt, right), rc.at[i, 0, lo], right), (blk_b(pt, left), rc.at[i, 1, hi], left))[kind]
        return rcopy(src, dst, rs_send.at[i, 4 + kind], rs_recv.at[i, 4 + kind], dev)

    def rs_add(i, who, extra, off=0, size=seq):
        where_rows = rows(who * seq + off, size)
        part[i, where_rows, :] = part[i, where_rows, :] + extra

    def rs_a(i):
        for role in range(4):
            rs_d2d(i, role).start()

    def rs_b(i):
        rs_d2d(i, 0).wait_recv()
        rs_add(i, opp, ra[i, 0])
        rs_ring(i, 0).start()
        rs_ring(i, 1).start()

    def rs_c(i):
        rs_d2d(i, 1).wait_recv()
        rs_add(i, right, ra[i, 1])
        rs_ring(i, 2).start()
        rs_d2d(i, 2).wait_recv()
        rs_add(i, left, ra[i, 2])
        rs_ring(i, 3).start()

    def rs_d(i):
        rs_ring(i, 0).wait_recv()
        rs_add(i, right, rb[i, 0], 0, half)
        rs_ring(i, 4).start()
        rs_ring(i, 1).wait_recv()
        rs_add(i, left, rb[i, 1], half, half)
        rs_ring(i, 5).start()

    def rs_e(i):
        rs_d2d(i, 3).wait_recv()
        for kind in range(2, 6):
            rs_ring(i, kind).wait_recv()
        for role in range(4):
            rs_d2d(i, role).wait_send()
        for kind in range(6):
            rs_ring(i, kind).wait_send()
        return (part[i, rows(me * seq), :] + ra[i, 3]) + (rc[i, 0] + rc[i, 1])

    bufs = (n2, cc, n1, ee)

    def ag_msg(i, kind, receive=False):
        buf = bufs[i]
        if receive:
            p_left = lax.rem(partner + tp - 2, tp)
            p_right = lax.rem(partner + 2, tp)
            p_opp = lax.rem(partner + chips, tp)
            ref = (lambda: blk(buf, left), lambda: blk(buf, right), lambda: blk(buf, partner), lambda: blk_a(buf, opp),
                   lambda: blk_b(buf, opp), lambda: blk(buf, p_left), lambda: blk(buf, p_right),
                   lambda: blk_a(buf, p_opp), lambda: blk_b(buf, p_opp))[kind]()
        else:
            ref = (lambda: blk(buf, me), lambda: blk(buf, me), lambda: blk(buf, me), lambda: blk_a(buf, left),
                   lambda: blk_b(buf, right), lambda: blk(buf, left), lambda: blk(buf, right),
                   lambda: blk_a(buf, opp), lambda: blk_b(buf, opp))[kind]()
        dev = (right, left, partner, right, left, partner, partner, partner, partner)[kind]
        return rcopy(ref, ref, ag_send.at[i, kind], ag_recv.at[i, kind], dev)

    def ag_f(i):
        for kind in range(3):
            ag_msg(i, kind).start()

    def ag_g(i):
        ag_msg(i, 0, True).wait_recv()
        ag_msg(i, 3).start()
        ag_msg(i, 5).start()
        ag_msg(i, 1, True).wait_recv()
        ag_msg(i, 4).start()
        ag_msg(i, 6).start()

    def ag_h(i):
        ag_msg(i, 3, True).wait_recv()
        ag_msg(i, 7).start()
        ag_msg(i, 4, True).wait_recv()
        ag_msg(i, 8).start()

    def ag_i(i):
        for kind in (2, 5, 6, 7, 8):
            ag_msg(i, kind, True).wait_recv()
        for kind in range(9):
            ag_msg(i, kind).wait_send()

    def out_copy(k, src, dst, layer):
        return pltpu.make_async_copy(src, dst.at[layer], out_sem.at[k])

    def rms(x_val):
        inv = lax.rsqrt(jnp.mean(x_val * x_val, axis=-1, keepdims=True) + EPS)
        return x_val * inv, inv

    barrier = pltpu.get_barrier_semaphore()
    for other in (partner, right, left):
        pl.semaphore_signal(barrier, inc=1, device_id={'tp': other}, device_id_type=MESH)
    loads = [pltpu.make_async_copy(y1_h, part.at[2], in_sem.at[0]),
             pltpu.make_async_copy(dy2_h, part.at[3], in_sem.at[1]),
             pltpu.make_async_copy(blk(y1_h, me), x1.at[1], in_sem.at[2]),
             pltpu.make_async_copy(blk(y2_h, me), x2.at[1], in_sem.at[3]),
             pltpu.make_async_copy(blk(dy1_h, me), dy1, in_sem.at[4]),
             pltpu.make_async_copy(blk(dy2_h, me), dy2, in_sem.at[5])]
    for cp in loads:
        cp.start()
    for cp in w_copies(0):
        cp.start()
    row_id = lax.broadcasted_iota(jnp.int32, (tokens, tokens), 0)
    col_id = lax.broadcasted_iota(jnp.int32, (tokens, tokens), 1)
    seen = jnp.zeros((tokens, tokens), F32)
    for b in range(tp):
        inside = (row_id < (b + 1) * seq) & (col_id >= b * seq) & (col_id <= row_id) & (col_id < b * seq + lens[b])
        seen = jnp.where(inside, 1.0, seen)
    mask[...] = seen
    loads[0].wait()

    @pl.loop(0, tp)
    def _(b):
        r = rows(b * seq)
        n1[r, :] = rms(part[2, r, :])[0].astype(BF16)
    loads[1].wait()

    @pl.loop(0, tp)
    def _(b):
        r = rows(b * seq)
        ee[r, :] = part[3, r, :].astype(BF16)
    for cp in loads[2:]:
        cp.wait()
    pl.semaphore_wait(barrier, 3)

    col_tile = 512

    def product(i, lhs_ref, w_ref):
        @pl.loop(0, width // col_tile)
        def _(j):
            cols = pl.ds(pl.multiple_of(j * col_tile, col_tile), col_tile)
            part[i, :, cols] = mm(lhs_ref[...], w_ref[:, cols], NN)

    @pl.loop(0, n_layers)
    def _(step):
        layer = n_layers - 1 - step
        slot = lax.rem(step, 2)
        other = 1 - slot
        w1_s, w2_s, wqkv_s, wo_s = w1.at[slot], w2.at[slot], wqkv.at[slot], wo.at[slot]
        later = step > 0
        more = step < n_layers - 1
        for cp in w_copies(step):
            cp.wait()

        @pl.when(more)
        def _():
            for cp in w_copies(step + 1):
                cp.start()

        @pl.when(later)
        def _():
            ag_i(2)
        out_copy(0, n1, n1_o, layer).start()
        pre = mm(n1[...], w1_s[...], NT)
        tan = jnp.tanh(GELU_C * (pre + GELU_A * (pre * pre * pre)))
        cdf = 0.5 * (1.0 + tan)
        h_s[...] = (pre * cdf).astype(BF16)
        gp[...] = cdf + pre * (0.5 * GELU_C) * (1.0 - tan * tan) * (1.0 + (3.0 * GELU_A) * (pre * pre))
        out_copy(1, h_s, h_o, layer).start()

        @pl.when(later)
        def _():
            ag_g(3)
        product(0, h_s, w2_s)
        rs_a(0)

        @pl.when(later)
        def _():
            ag_h(3)
        rs_b(0)

        @pl.when(later)
        def _():
            ag_i(3)
        out_copy(2, ee, e_o, layer).start()
        rs_c(0)
        u_s[...] = (gp[...] * mm(ee[...], w2_s[...], NT)).astype(BF16)
        out_copy(3, u_s, u_o, layer).start()
        product(1, u_s, w1_s)
        rs_a(1)
        rs_d(0)
        rs_b(1)
        rs_c(1)
        total = rs_e(0)
        x2_new = x2[other] - total
        x2[slot] = x2_new
        n2[rows(me * seq), :] = rms(x2_new)[0].astype(BF16)
        ag_f(0)
        rs_d(1)
        ag_g(0)
        ag_h(0)
        total = rs_e(1)
        norm, inv = rms(x1[other])
        dy1_new = dy1[...] + inv * (total - norm * jnp.mean(total * norm, axis=-1, keepdims=True))
        dy1[...] = dy1_new
        cc[rows(me * seq), :] = dy1_new.astype(BF16)
        ag_f(1)
        ag_i(0)
        out_copy(4, n2, n2_o, layer).start()
        qkv[...] = mm(n2[...], wqkv_s[...], NT).astype(BF16)
        ag_g(1)
        key, val = qkv[:, qw:qw + hd], qkv[:, qw + hd:qw + 2 * hd]
        for r in range(heads):
            sc = mm(qkv[:, r * hd:(r + 1) * hd], key, NT) * scale
            sc = jnp.where(mask[...] > 0.5, sc, MASK_VALUE)
            ex = jnp.exp(sc - jnp.max(sc, axis=-1, keepdims=True))
            pr = ex / jnp.sum(ex, axis=-1, keepdims=True)
            probs[r] = pr
            att[:, r * hd:(r + 1) * hd] = mm(pr.astype(BF16), val, NN).astype(BF16)
        out_copy(5, att, a_o, layer).start()
        ag_h(1)
        product(2, att, wo_s)
        out_copy(0, n1, n1_o, layer).wait()
        rs_a(2)
        rs_b(2)
        rs_c(2)
        ag_i(1)
        out_copy(6, cc, c_o, layer).start()
        d_att = mm(cc[...], wo_s[...], NT).astype(BF16)
        d_key = jnp.zeros((tokens, hd), F32)
        d_val = jnp.zeros((tokens, hd), F32)
        for r in range(heads):
            da = d_att[:, r * hd:(r + 1) * hd]
            pr = probs[r]
            dp = mm(da, val, NT)
            ds = (pr * (dp - jnp.sum(dp * pr, axis=-1, keepdims=True)) * scale).astype(BF16)
            dqkv[:, r * hd:(r + 1) * hd] = mm(ds, key, NN).astype(BF16)
            d_key = d_key + mm(ds, qkv[:, r * hd:(r + 1) * hd], TN)
            d_val = d_val + mm(pr.astype(BF16), da, TN)
        dqkv[:, qw:qw + hd] = d_key.astype(BF16)
        dqkv[:, qw + hd:qw + 2 * hd] = d_val.astype(BF16)
        out_copy(7, dqkv, d_o, layer).start()
        rs_d(2)
        product(3, dqkv, wqkv_s)
        out_copy(2, ee, e_o, layer).wait()
        rs_a(3)
        rs_b(3)
        rs_c(3)
        total = rs_e(2)
        x1_new = x1[other] - total
        x1[slot] = x1_new
        n1[rows(me * seq), :] = rms(x1_new)[0].astype(BF16)

        @pl.when(more)
        def _():
            ag_f(2)
        rs_d(3)

        @pl.when(more)
        def _():
            ag_g(2)
            ag_h(2)
        total = rs_e(3)
        norm, inv = rms(x2[slot])
        dy2_new = dy2[...] + inv * (total - norm * jnp.mean(total * norm, axis=-1, keepdims=True))
        dy2[...] = dy2_new
        ee[rows(me * seq), :] = dy2_new.astype(BF16)

        @pl.when(more)
        def _():
            ag_f(3)
        for k, src, dst in ((1, h_s, h_o), (3, u_s, u_o), (4, n2, n2_o), (5, att, a_o), (6, cc, c_o), (7, dqkv, d_o)):
            out_copy(k, src, dst, layer).wait()

    last = (n_layers - 1) % 2
    finals = [pltpu.make_async_copy(src, fin_h.at[k], fin_sem.at[k])
              for k, src in enumerate((x1.at[last], x2.at[last], dy1, dy2))]
    for cp in finals:
        cp.start()
    for cp in finals:
        cp.wait()


def solution(mesh):
    tp = mesh.shape['tp']
    assert tp == 8
    act_spec = P('dp', None, None)
    w_specs = (P(None, None, 'tp', None), P(None, None, 'tp', None), P(None, None, 'tp', None),
               P(None, 'tp', None, None), P(None, None, 'tp'), P(None, 'tp', None))
    g_specs = (P('dp', None, 'tp', None), P('dp', None, 'tp', None), P('dp', None, 'tp', None),
               P('dp', 'tp', None, None), P('dp', None, 'tp'), P('dp', 'tp', None))

    def local_fn(y_one, y_two, dy_one, dy_two, seq_lens, w_query, w_key, w_value, w_out, w_up, w_down):
        batch, seq, width = y_one.shape
        n_layers, _, heads, hd = w_query.shape
        assert batch == tp and w_key.shape[2] == 1
        tokens = batch * seq
        ff = w_down.shape[1]
        qw = heads * hd
        half = seq // 2
        acts = [x.reshape(tokens, width) for x in (y_one, y_two, dy_one, dy_two)]

        def flip(w):
            return w.transpose(0, 2, 3, 1).reshape(n_layers, -1, width)
        weights = (w_up.transpose(0, 2, 1), w_down, flip(w_query), flip(w_key), flip(w_value), w_out.reshape(n_layers, qw, width))

        def stack(cols):
            return jax.ShapeDtypeStruct((n_layers, tokens, cols), BF16)
        any_spec = pl.BlockSpec(memory_space=pl.ANY)
        vm = pltpu.VMEM
        dma = pltpu.SemaphoreType.DMA
        scratch = [vm((tokens, width), BF16)] * 4 + [
            vm((2, ff, width), BF16), vm((2, ff, width), BF16), vm((2, qw + 2 * hd, width), BF16), vm((2, qw, width), BF16),
            vm((tokens, ff), BF16), vm((tokens, ff), BF16), vm((tokens, ff), F32),
            vm((tokens, qw + 2 * hd), BF16), vm((tokens, qw), BF16), vm((tokens, qw + 2 * hd), BF16),
            vm((heads, tokens, tokens), F32), vm((tokens, tokens), F32),
            vm((2, seq, width), F32), vm((2, seq, width), F32), vm((seq, width), F32), vm((seq, width), F32),
            vm((4, tokens, width), F32), vm((4, 4, seq, width), F32), vm((4, 2, half, width), F32), vm((4, 2, seq, width), F32),
            dma((2, 6)), dma((6,)), dma((8,)), dma((4,)), dma((4, 10)), dma((4, 10)), dma((4, 9)), dma((4, 9))]
        fin, n1, n2, c_val, e_val, h_val, u_val, a_val, d_val = pl.pallas_call(
            functools.partial(chain_kernel, (n_layers, tp, seq, width, heads, hd)),
            out_shape=(jax.ShapeDtypeStruct((4, seq, width), F32), stack(width), stack(width), stack(width), stack(width),
                       stack(ff), stack(ff), stack(qw), stack(qw + 2 * hd)),
            in_specs=[pl.BlockSpec(memory_space=pltpu.SMEM)] + [any_spec] * 10,
            out_specs=(any_spec,) * 9,
            scratch_shapes=scratch,
            compiler_params=pltpu.CompilerParams(collective_id=0, has_side_effects=True, vmem_limit_bytes=66_000_000),
            name='chain',
        )(seq_lens, *acts, *weights)

        def grad(small, wide):
            return jnp.einsum('lts,ltd->lsd', small, wide, preferred_element_type=F32)
        dw_up = grad(u_val, n1).transpose(0, 2, 1)
        dw_down = grad(h_val, e_val)
        dw_out = grad(a_val, c_val).reshape(w_out.shape)

        def flip_back(g, like):
            return g.reshape(n_layers, -1, hd, width).transpose(0, 3, 1, 2).reshape(like.shape)
        dw_query = flip_back(grad(d_val[:, :, :qw], n2), w_query)
        dw_key = flip_back(grad(d_val[:, :, qw:qw + hd], n2), w_key)
        dw_value = flip_back(grad(d_val[:, :, qw + hd:], n2), w_value)
        ends = tuple(lax.all_gather(fin[k:k + 1], 'tp', axis=0, tiled=True) for k in range(4))
        return ends + (dw_query, dw_key, dw_value, dw_out, dw_up, dw_down)

    return jax.shard_map(local_fn, mesh=mesh,
                         in_specs=(act_spec,) * 4 + (P('dp'),) + w_specs,
                         out_specs=(act_spec,) * 4 + g_specs,
                         check_vma=False)
```

time: 706 us -> 386 us (0.55); the launches traced: 695 us -> 386 us
  waiting for transfers between devices: 423 us -> 54 us
  Pallas kernels: 0 us -> 270 us
  matrix products: 141 us -> 37.7 us
  other arithmetic: 77.6 us -> 0 us
  local copies, waits for them, and re-layouts: 36 us -> 10.3 us
    psum x8 -> x0, waiting for transfers between devices: 423 us -> none  [tp_sum(): return lax.psum(partial_val, 'tp')]
    pallas_call x0 -> x1, Pallas kernels: none -> 270 us  [local_fn(): pl.pallas_call(functools.partial(chain_kernel, (n_layers, tp, seq, width,...]
    dot_general x96 -> x6, matrix products: 141 us -> 37.7 us  [grad(): return jnp.einsum('lts,ltd->lsd', small, wide, preferred_element_type=F32)]
    all_gather x0 -> x4, waiting for transfers between devices: none -> 52.1 us  [local_fn(): lax.all_gather(fin[k:k + 1], 'tp', axis=0, tiled=True)]
    another operation x10 -> x0, other arithmetic: 40.7 us -> none  [the longest x6 40.1 us: stack_grads(): jnp.stack([layer_grads[grad_pos] for layer_grads in grads_by_layer])]
    unnamed x224 -> x24, local copies, waits for them, and re-layouts: 36 us -> 8.12 us
    reduce_sum x20 -> x0, other arithmetic: 26.6 us -> none  [the longest x8 13.3 us: rms_norm(): inv_rms = lax.rsqrt(jnp.mean(x_val * x_val, axis=-1, keepdims=True) + EPS)]
    add x7 -> x0, other arithmetic: 7.83 us -> none  [the longest x4 6.53 us: block_back(): dx_two = dy_two + rms_back(norm_f, inv_f, grad_norm_f)]
  transfers between devices with their start and end apart: 8 -> 4, of which waited for: 8 -> 3; matrix products, arithmetic and copies ran while one was open for 12% -> 10% of each run, Pallas kernels for 0% -> 0%
where the time goes in v1:
time: 386 us
  Pallas kernels  270 us (70%)
  waiting for transfers between devices  54 us (14%)
  matrix products  37.7 us (10%)
  between operations  13.8 us (4%)
  local copies, waits for them, and re-layouts  10.3 us (3%)
    pallas_call x1, Pallas kernels, local_fn(): pl.pallas_call(functools.partial(chain_kernel, (n_layers, tp, seq, width,...  270 us
    all_gather x4, waiting for transfers between devices, local_fn(): lax.all_gather(fin[k:k + 1], 'tp', axis=0, tiled=True)  52.1 us
    dot_general x6, matrix products, grad(): return jnp.einsum('lts,ltd->lsd', small, wide, preferred_element_type=F32)  37.7 us
    unnamed x24, local copies, waits for them, and re-layouts  8.12 us
  transfers between devices with their start and end apart: 4, of which 3 were waited for; matrix products, arithmetic and copies ran while one was open for 10% of the time, Pallas kernels for 0%

profile of v1, /device:TPU:113, one launch (start us, length us, event | category | flops | bytes accessed | tf_op | source)
XLA Modules:
  0.0 386.2 jit_solution(6218875764774033044)
XLA Ops:
  7.2 0.1 all-gather.5.cloned.1.call-start
  7.3 270.0 %chain.1 = (f32[4,32,2048]{2,1,0:T(8,128)}, bf16[4,256,2048]{2,1,0:T(8,128)(2,1)}, bf16[4,256,2048]{2,1,0:T(8,128)(2,1)}, bf16[4,256,2048]{2,1,0:T(8,128)(2,1)},...) custom-call(s32[8]{0:T(128)} %lens.1, ...), custom_call_target="tpu_custom_call" | custom-call | tf_op jit(solution)/shard_map/chain/pallas_call | solution.py:396
  277.3 2.2 fusion.4
  279.4 0.1 all-gather.5.cloned.1.call-update
  279.5 0.1 all-gather.7.cloned.1.call-start
  279.6 0.7 all-gather.7.cloned.1.call-update
  280.3 0.1 all-gather.9.cloned.1.call-start
  280.4 0.7 all-gather.9.cloned.1.call-update
  281.1 0.2 all-gather.11.cloned.1.call-start
  281.3 0.4 all-gather.11.cloned.1.call-update
  281.7 0.0 copy-start
  281.7 0.0 copy-start.5
  281.8 4.7 %convolution_bitcast_fusion = f32[4,2048,1,64]{1,3,2,0:T(8,128)} fusion(bf16[4,256,2048]{2,1,0:T(8,128)(2,1)} %get-tuple-element.21, bf16[4,256,384]{2,1,0:T(8,128)(2,1)} %get-tuple-element.20), kind=kOutput, calls=%fused_computation | convolution fusion | flops 268435456 | bytes 6553600 | tf_op jit(solution)/shard_map/lts,ltd->lsd/dot_general | solution.py:408
  286.5 0.0 copy-done
  286.5 0.0 copy-done.5
  286.5 4.7 %fusion = f32[4,256,2048]{2,1,0:T(8,128)} fusion(bf16[4,256,2048]{2,1,0:T(8,128)(2,1)S(1)} %copy-done, bf16[4,256,384]{2,1,0:T(8,128)(2,1)S(1)} %copy-done.5), kind=kOutput, calls=%fused_computation.2 | convolution fusion | flops 1073741824 | bytes 13107200 | tf_op jit(solution)/shard_map/lts,ltd->lsd/dot_general | solution.py:408
  291.2 2.2 convolution_bitcast_fusion.1
  293.4 0.7 copy-done.3
  294.1 0.1 copy-done.9
  294.2 4.7 %fusion.5 = f32[4,256,2048]{2,1,0:T(8,128)} fusion(bf16[4,256,256]{2,1,0:T(8,128)(2,1)S(1)} %copy-done.9, bf16[4,256,2048]{2,1,0:T(8,128)(2,1)S(1)} %copy-done.3), kind=kOutput, calls=%fused_computation.7 | convolution fusion | flops 1073741824 | bytes 13107200 | tf_op jit(solution)/shard_map/lts,ltd->lsd/dot_general | solution.py:408
  299.0 0.0 copy-done.1
  299.0 0.0 copy-done.4
  299.0 10.0 %fusion.6 = f32[4,2048,704]{1,2,0:T(8,128)} fusion(bf16[4,256,2048]{2,1,0:T(8,128)(2,1)S(1)} %copy-done.1, bf16[4,256,704]{2,1,0:T(8,128)(2,1)S(1)} %copy-done.4), kind=kOutput, calls=%fused_computation.8 | convolution fusion | flops 2952790016 | bytes 28704768 | tf_op jit(solution)/shard_map/lts,ltd->lsd/dot_general | solution.py:408
  309.0 0.0 copy-done.2
  309.0 11.4 %fusion.7 = f32[4,704,2048]{2,1,0:T(8,128)} fusion(bf16[4,256,704]{2,1,0:T(8,128)(2,1)} %get-tuple-element.26, bf16[4,256,2048]{2,1,0:T(8,128)(2,1)S(1)} %copy-done.2), kind=kOutput, calls=%fused_computation.9 | convolution fusion | flops 2952790016 | bytes 28704768 | tf_op jit(solution)/shard_map/lts,ltd->lsd/dot_general | solution.py:408
  320.3 4.7 %all-gather.7.cloned.1.call-done = f32[8,32,2048]{2,1,0:T(8,128)} async-done(((f32[1,32,2048]{2,1,0:T(8,128)}), f32[8,32,2048]{2,1,0:T(8,128)}) %all-gather.7.cloned.1.call-update) | async-done | bytes 2097168 | tf_op jit(solution)/shard_map/all_gather | solution.py:418
  325.0 23.8 %all-gather.9.cloned.1.call-done = f32[8,32,2048]{2,1,0:T(8,128)} async-done(((f32[1,32,2048]{2,1,0:T(8,128)}), f32[8,32,2048]{2,1,0:T(8,128)}) %all-gather.9.cloned.1.call-update) | async-done | bytes 2097168 | tf_op jit(solution)/shard_map/all_gather | solution.py:418
  348.8 23.6 %all-gather.11.cloned.1.call-done = f32[8,32,2048]{2,1,0:T(8,128)} async-done(((f32[1,32,2048]{2,1,0:T(8,128)}), f32[8,32,2048]{2,1,0:T(8,128)}) %all-gather.11.cloned.1.call-update) | async-done | bytes 2097168 | tf_op jit(solution)/shard_map/all_gather | solution.py:418
  372.4 3.3 copy.51
  375.7 1.3 copy.52
  377.0 1.3 copy.53
  378.4 1.3 copy.54
  (12 shorter events, 0.0 us)
Async XLA Ops:
  7.2 313.1 %all-gather.5.cloned.1.call-start = ((), (), s32[]{:S(2)}) async-start(), calls=%async_computation | async-start | bytes 2359296 | tf_op jit(solution)/shard_map/all_gather | solution.py:418
  279.5 45.5 %all-gather.7.cloned.1.call-start = ((), (), s32[]{:S(2)}) async-start(), calls=%async_computation.1 | async-start | bytes 2359296 | tf_op jit(solution)/shard_map/all_gather | solution.py:418
  280.3 68.5 %all-gather.9.cloned.1.call-start = ((), (), s32[]{:S(2)}) async-start(), calls=%async_computation.2 | async-start | bytes 2359296 | tf_op jit(solution)/shard_map/all_gather | solution.py:418
  281.1 91.3 %all-gather.11.cloned.1.call-start = ((), (), s32[]{:S(2)}) async-start(), calls=%async_computation.3 | async-start | bytes 2359296 | tf_op jit(solution)/shard_map/all_gather | solution.py:418
  281.7 4.7 %copy-start = (bf16[4,256,2048]{2,1,0:T(8,128)(2,1)S(1)}, bf16[4,256,2048]{2,1,0:T(8,128)(2,1)}, u32[]{:S(2)}) copy-start(bf16[4,256,2048]{2,1,0:T(8,128)(2,1)} %get-tuple-element.21) | copy-start | bytes 12582916
  281.7 4.7 %copy-start.5 = (bf16[4,256,384]{2,1,0:T(8,128)(2,1)S(1)}, bf16[4,256,384]{2,1,0:T(8,128)(2,1)}, u32[]{:S(2)}) copy-start(bf16[4,256,384]{2,1,0:T(8,128)(2,1)} %get-tuple-element.20) | copy-start | bytes 2359300
  291.2 2.9 copy-start.3
  291.2 3.1 copy-start.9
  294.2 4.7 %copy-start.1 = (bf16[4,256,2048]{2,1,0:T(8,128)(2,1)S(1)}, bf16[4,256,2048]{2,1,0:T(8,128)(2,1)}, u32[]{:S(2)}) copy-start(bf16[4,256,2048]{2,1,0:T(8,128)(2,1)} %get-tuple-element.24) | copy-start | bytes 12582916
  294.2 4.7 %copy-start.4 = (bf16[4,256,704]{2,1,0:T(8,128)(2,1)S(1)}, bf16[4,256,704]{2,1,0:T(8,128)(2,1)}, u32[]{:S(2)}) copy-start(bf16[4,256,704]{2,1,0:T(8,128)(2,1)} %get-tuple-element.25) | copy-start | bytes 4325380
  299.0 10.0 %copy-start.2 = (bf16[4,256,2048]{2,1,0:T(8,128)(2,1)S(1)}, bf16[4,256,2048]{2,1,0:T(8,128)(2,1)}, u32[]{:S(2)}) copy-start(bf16[4,256,2048]{2,1,0:T(8,128)(2,1)} %get-tuple-element.27) | copy-start | bytes 12582916
  325.0 50.7 %copy-start.6 = (f32[8,32,2048]{2,1,0:T(8,128)S(1)}, f32[8,32,2048]{2,1,0:T(8,128)}, u32[]{:S(2)}) copy-start(f32[8,32,2048]{2,1,0:T(8,128)} %all-gather.7.cloned.1.call-done) | copy-start | bytes 6291460
  372.4 4.6 %copy-start.7 = (f32[8,32,2048]{2,1,0:T(8,128)S(1)}, f32[8,32,2048]{2,1,0:T(8,128)}, u32[]{:S(2)}) copy-start(f32[8,32,2048]{2,1,0:T(8,128)} %all-gather.9.cloned.1.call-done) | copy-start | bytes 6291460
  375.7 2.6 copy-start.8
Sparse Core Ops, SparseCore 0:
  279.6 21.5 all-gather.4
  303.4 21.5 all-gather.6
  327.2 21.5 all-gather.8
  350.8 21.5 all-gather.10

commit v2 on v1

--- a/solution.py
+++ b/solution.py
@@ -24,9 +24,9 @@
 
 
 def chain_kernel(cfg, lens, y1_h, y2_h, dy1_h, dy2_h, w1_h, w2_h, wq_h, wk_h, wv_h, wo_h,
-                 fin_h, n1_o, n2_o, c_o, e_o, h_o, u_o, a_o, d_o,
+                 f_x1, f_x2, f_dy1, f_dy2, n1_o, n2_o, c_o, e_o, h_o, u_o, a_o, d_o,
                  n1, n2, cc, ee, w1, w2, wqkv, wo, h_s, u_s, gp, qkv, att, dqkv, probs, mask,
-                 x1, x2, dy1, dy2, part, ra, rb, rc,
+                 x1, x2, dy1, dy2, part, ra, rb, rc, fbuf,
                  w_sem, in_sem, out_sem, fin_sem, rs_send, rs_recv, ag_send, ag_recv):
     n_layers, tp, seq, width, heads, hd = cfg
     chips = tp // 2
@@ -124,7 +124,8 @@
             rs_ring(i, kind).wait_send()
         return (part[i, rows(me * seq), :] + ra[i, 3]) + (rc[i, 0] + rc[i, 1])
 
-    bufs = (n2, cc, n1, ee)
+    bufs = (n2, cc, n1, ee, fbuf.at[0], fbuf.at[1], fbuf.at[2], fbuf.at[3])
+    f_out = (f_x1, f_x2, f_dy1, f_dy2)
 
     def ag_msg(i, kind, receive=False):
         buf = bufs[i]
@@ -165,6 +166,17 @@
             ag_msg(i, kind, True).wait_recv()
         for kind in range(9):
             ag_msg(i, kind).wait_send()
+
+    def fin_start(k, value):
+        fbuf[k, rows(me * seq), :] = value
+        ag_f(4 + k)
+
+    def fin_copy(k):
+        return pltpu.make_async_copy(fbuf.at[k], f_out[k], fin_sem.at[k])
+
+    def fin_end(k):
+        ag_i(4 + k)
+        fin_copy(k).start()
 
     def out_copy(k, src, dst, layer):
         return pltpu.make_async_copy(src, dst.at[layer], out_sem.at[k])
@@ -225,6 +237,7 @@
         w1_s, w2_s, wqkv_s, wo_s = w1.at[slot], w2.at[slot], wqkv.at[slot], wo.at[slot]
         later = step > 0
         more = step < n_layers - 1
+        end = step == n_layers - 1
         for cp in w_copies(step):
             cp.wait()
 
@@ -295,12 +308,24 @@
             att[:, r * hd:(r + 1) * hd] = mm(pr.astype(BF16), val, NN).astype(BF16)
         out_copy(5, att, a_o, layer).start()
         ag_h(1)
+
+        @pl.when(end)
+        def _():
+            fin_start(1, x2[slot])
         product(2, att, wo_s)
         out_copy(0, n1, n1_o, layer).wait()
         rs_a(2)
         rs_b(2)
+
+        @pl.when(end)
+        def _():
+            ag_g(5)
         rs_c(2)
         ag_i(1)
+
+        @pl.when(end)
+        def _():
+            fin_start(2, dy1[...])
         out_copy(6, cc, c_o, layer).start()
         d_att = mm(cc[...], wo_s[...], NT).astype(BF16)
         d_key = jnp.zeros((tokens, hd), F32)
@@ -317,11 +342,20 @@
         dqkv[:, qw + hd:qw + 2 * hd] = d_val.astype(BF16)
         out_copy(7, dqkv, d_o, layer).start()
         rs_d(2)
+
+        @pl.when(end)
+        def _():
+            ag_h(5)
+            ag_g(6)
         product(3, dqkv, wqkv_s)
         out_copy(2, ee, e_o, layer).wait()
         rs_a(3)
         rs_b(3)
         rs_c(3)
+
+        @pl.when(end)
+        def _():
+            ag_h(6)
         total = rs_e(2)
         x1_new = x1[other] - total
         x1[slot] = x1_new
@@ -330,12 +364,23 @@
         @pl.when(more)
         def _():
             ag_f(2)
+
+        @pl.when(end)
+        def _():
+            fin_start(0, x1_new)
         rs_d(3)
 
         @pl.when(more)
         def _():
             ag_g(2)
             ag_h(2)
+
+        @pl.when(end)
+        def _():
+            fin_end(1)
+            fin_end(2)
+            ag_g(4)
+            ag_h(4)
         total = rs_e(3)
         norm, inv = rms(x2[slot])
         dy2_new = dy2[...] + inv * (total - norm * jnp.mean(total * norm, axis=-1, keepdims=True))
@@ -345,16 +390,30 @@
         @pl.when(more)
         def _():
             ag_f(3)
+
+        @pl.when(end)
+        def _():
+            fin_start(3, dy2_new)
         for k, src, dst in ((1, h_s, h_o), (3, u_s, u_o), (4, n2, n2_o), (5, att, a_o), (6, cc, c_o), (7, dqkv, d_o)):
             out_copy(k, src, dst, layer).wait()
 
-    last = (n_layers - 1) % 2
-    finals = [pltpu.make_async_copy(src, fin_h.at[k], fin_sem.at[k])
-              for k, src in enumerate((x1.at[last], x2.at[last], dy1, dy2))]
-    for cp in finals:
-        cp.start()
-    for cp in finals:
-        cp.wait()
+    ag_g(7)
+    ag_h(7)
+    fin_end(0)
+    fin_end(3)
+    for k in range(4):
+        fin_copy(k).wait()
+
+
+def grad_kernel(parts, n1, n2, c_val, e_val, h_val, u_val, a_val, d_val, g_up, g_down, g_q, g_k, g_v, g_out):
+    qw, hd = parts
+    g_up[0] = mm(u_val[0], n1[0], TN)
+    g_down[0] = mm(h_val[0], e_val[0], TN)
+    g_out[0] = mm(a_val[0], c_val[0], TN)
+    g_all = mm(d_val[0], n2[0], TN)
+    g_q[0] = g_all[:qw]
+    g_k[0] = g_all[qw:qw + hd]
+    g_v[0] = g_all[qw + hd:]
 
 
 def solution(mesh):
@@ -392,30 +451,44 @@
             vm((heads, tokens, tokens), F32), vm((tokens, tokens), F32),
             vm((2, seq, width), F32), vm((2, seq, width), F32), vm((seq, width), F32), vm((seq, width), F32),
             vm((4, tokens, width), F32), vm((4, 4, seq, width), F32), vm((4, 2, half, width), F32), vm((4, 2, seq, width), F32),
-            dma((2, 6)), dma((6,)), dma((8,)), dma((4,)), dma((4, 10)), dma((4, 10)), dma((4, 9)), dma((4, 9))]
-        fin, n1, n2, c_val, e_val, h_val, u_val, a_val, d_val = pl.pallas_call(
+            vm((4, tokens, width), F32),
+            dma((2, 6)), dma((6,)), dma((8,)), dma((4,)), dma((4, 10)), dma((4, 10)), dma((8, 9)), dma((8, 9))]
+        *ends, n1, n2, c_val, e_val, h_val, u_val, a_val, d_val = pl.pallas_call(
             functools.partial(chain_kernel, (n_layers, tp, seq, width, heads, hd)),
-            out_shape=(jax.ShapeDtypeStruct((4, seq, width), F32), stack(width), stack(width), stack(width), stack(width),
+            out_shape=(jax.ShapeDtypeStruct((tokens, width), F32),) * 4 + (stack(width), stack(width), stack(width), stack(width),
                        stack(ff), stack(ff), stack(qw), stack(qw + 2 * hd)),
             in_specs=[pl.BlockSpec(memory_space=pltpu.SMEM)] + [any_spec] * 10,
-            out_specs=(any_spec,) * 9,
+            out_specs=(any_spec,) * 12,
             scratch_shapes=scratch,
             compiler_params=pltpu.CompilerParams(collective_id=0, has_side_effects=True, vmem_limit_bytes=66_000_000),
             name='chain',
         )(seq_lens, *acts, *weights)
 
-        def grad(small, wide):
-            return jnp.einsum('lts,ltd->lsd', small, wide, preferred_element_type=F32)
-        dw_up = grad(u_val, n1).transpose(0, 2, 1)
-        dw_down = grad(h_val, e_val)
-        dw_out = grad(a_val, c_val).reshape(w_out.shape)
+        col_tile = 512
+
+        def wide():
+            return pl.BlockSpec((1, tokens, col_tile), lambda layer, j: (layer, 0, j))
+
+        def small(cols):
+            return pl.BlockSpec((1, tokens, cols), lambda layer, j: (layer, 0, 0))
+        g_rows = (ff, ff, qw, hd, hd, qw)
+        moved = 2 * n_layers * tokens * (4 * width + 2 * ff + 2 * qw + 2 * hd) + 4 * n_layers * width * sum(g_rows)
+        g_up, g_down, g_q, g_k, g_v, g_out = pl.pallas_call(
+            functools.partial(grad_kernel, (qw, hd)),
+            grid=(n_layers, width // col_tile),
+            out_shape=tuple(jax.ShapeDtypeStruct((n_layers, r, width), F32) for r in g_rows),
+            in_specs=[wide()] * 4 + [small(ff), small(ff), small(qw), small(qw + 2 * hd)],
+            out_specs=tuple(pl.BlockSpec((1, r, col_tile), lambda layer, j: (layer, 0, j)) for r in g_rows),
+            compiler_params=pltpu.CompilerParams(vmem_limit_bytes=60_000_000),
+            cost_estimate=pl.CostEstimate(flops=2 * n_layers * tokens * width * sum(g_rows), bytes_accessed=moved, transcendentals=0),
+            name='grads',
+        )(n1, n2, c_val, e_val, h_val, u_val, a_val, d_val)
 
         def flip_back(g, like):
             return g.reshape(n_layers, -1, hd, width).transpose(0, 3, 1, 2).reshape(like.shape)
-        dw_query = flip_back(grad(d_val[:, :, :qw], n2), w_query)
-        dw_key = flip_back(grad(d_val[:, :, qw:qw + hd], n2), w_key)
-        dw_value = flip_back(grad(d_val[:, :, qw + hd:], n2), w_value)
-        ends = tuple(lax.all_gather(fin[k:k + 1], 'tp', axis=0, tiled=True) for k in range(4))
+        dw_up, dw_down, dw_out = g_up.transpose(0, 2, 1), g_down, g_out.reshape(w_out.shape)
+        dw_query, dw_key, dw_value = flip_back(g_q, w_query), flip_back(g_k, w_key), flip_back(g_v, w_value)
+        ends = tuple(v.reshape(batch, seq, width) for v in ends)
         return ends + (dw_query, dw_key, dw_value, dw_out, dw_up, dw_down)
 
     return jax.shard_map(local_fn, mesh=mesh,

time: 386 us -> 346 us (0.90)
  Pallas kernels: 270 us -> 336 us
  waiting for transfers between devices: 54 us -> 0 us
  matrix products: 37.7 us -> 0 us
  between operations: 13.8 us -> 0.69 us
    all_gather x4 -> x0, waiting for transfers between devices: 52.1 us -> none  [local_fn(): lax.all_gather(fin[k:k + 1], 'tp', axis=0, tiled=True)]
    dot_general x6 -> x0, matrix products: 37.7 us -> none  [grad(): return jnp.einsum('lts,ltd->lsd', small, wide, preferred_element_type=F32)]
    pallas_call x1, Pallas kernels: 270 us -> 306 us  [local_fn(): pl.pallas_call(functools.partial(chain_kernel, (n_layers, tp, seq, width,...]
    pallas_call x0 -> x1, Pallas kernels: none -> 30.1 us  [local_fn(): pl.pallas_call(functools.partial(grad_kernel, (qw, hd)), grid=(n_layers,...]
    unnamed x24 -> x12, local copies, waits for them, and re-layouts: 8.12 us -> 8.36 us
  transfers between devices with their start and end apart: 4 -> 0, of which waited for: 3 -> 0; matrix products, arithmetic and copies ran while one was open for 10% -> 0% of each run, Pallas kernels for 0% -> 0%
where the time goes in v2:
time: 346 us; the launch traced here: 345 us
  Pallas kernels  336 us (97%)
  local copies, waits for them, and re-layouts  8.36 us (2%)
    pallas_call x1, Pallas kernels, local_fn(): pl.pallas_call(functools.partial(chain_kernel, (n_layers, tp, seq, width,...  306 us
    pallas_call x1, Pallas kernels, local_fn(): pl.pallas_call(functools.partial(grad_kernel, (qw, hd)), grid=(n_layers,...  30.1 us
    unnamed x12, local copies, waits for them, and re-layouts  8.36 us

profile of v2, /device:TPU:113, one launch (start us, length us, event | category | flops | bytes accessed | tf_op | source)
XLA Modules:
  0.0 345.5 jit_solution(16496635156215293077)
XLA Ops:
  0.6 306.4 %chain.1 = (f32[256,2048]{1,0:T(8,128)}, f32[256,2048]{1,0:T(8,128)}, f32[256,2048]{1,0:T(8,128)}, f32[256,2048]{1,0:T(8,128)}, bf16[4,256,2048]{2,1,0:T(8,128)(...) custom-call(s32[8]{0:T(128)} %lens.1, ...), custom_call_target="tpu_custom_call" | custom-call | tf_op jit(solution)/shard_map/chain/pallas_call | solution.py:456
  307.0 0.0 copy-start.3
  307.0 30.1 %grads.1 = (f32[4,704,2048]{2,1,0:T(8,128)}, f32[4,704,2048]{2,1,0:T(8,128)}, f32[4,256,2048]{2,1,0:T(8,128)}, f32[4,64,2048]{2,1,0:T(8,128)}, f32[4,64,2048]{2,1,0:T(8,128)}, /*index=5*/f32[4,256,2048]{2,1,0:T(8,128)}) custom-call(bf16[4,256,2048]{2,1,0:T(8,128)(2,1)} %get-tuple-element.32.n1, bf16[4,256,2048]{2,1,0:T(8,128)(2,1)} %get-tuple-element.33.n2, ...), custom_call_target="tpu_custom_call" | custom-call | flops 8589934592 | bytes 88080384 | tf_op jit(solution)/shard_map/grads/pallas_call | solution.py:476
  337.1 0.0 copy-done.3
  337.1 0.0 copy-start.2
  337.1 1.3 copy.29
  338.4 1.0 copy-done.2
  339.5 0.0 copy-start.1
  339.5 1.3 copy.30
  340.8 1.0 copy-done.1
  341.8 0.0 copy-start
  341.8 1.3 copy.31
  343.1 1.0 copy-done
  344.2 1.3 copy.32
Async XLA Ops:
  307.0 30.1 %copy-start.3 = (f32[256,2048]{1,0:T(8,128)S(1)}, f32[256,2048]{1,0:T(8,128)}, u32[]{:S(2)}) copy-start(f32[256,2048]{1,0:T(8,128)} %get-tuple-element.28) | copy-start | bytes 6291460
  337.1 2.3 copy-start.2
  339.5 2.3 copy-start.1
  341.8 2.3 copy-start

commit v3 on v2

--- a/solution.py
+++ b/solution.py
@@ -194,31 +194,15 @@
              pltpu.make_async_copy(blk(y2_h, me), x2.at[1], in_sem.at[3]),
              pltpu.make_async_copy(blk(dy1_h, me), dy1, in_sem.at[4]),
              pltpu.make_async_copy(blk(dy2_h, me), dy2, in_sem.at[5])]
-    for cp in loads:
+    first = w_copies(0)
+    for cp in (loads[0], first[0], loads[1], first[1], *loads[2:], *first[2:]):
         cp.start()
-    for cp in w_copies(0):
-        cp.start()
-    row_id = lax.broadcasted_iota(jnp.int32, (tokens, tokens), 0)
-    col_id = lax.broadcasted_iota(jnp.int32, (tokens, tokens), 1)
-    seen = jnp.zeros((tokens, tokens), F32)
-    for b in range(tp):
-        inside = (row_id < (b + 1) * seq) & (col_id >= b * seq) & (col_id <= row_id) & (col_id < b * seq + lens[b])
-        seen = jnp.where(inside, 1.0, seen)
-    mask[...] = seen
     loads[0].wait()
 
     @pl.loop(0, tp)
     def _(b):
         r = rows(b * seq)
         n1[r, :] = rms(part[2, r, :])[0].astype(BF16)
-    loads[1].wait()
-
-    @pl.loop(0, tp)
-    def _(b):
-        r = rows(b * seq)
-        ee[r, :] = part[3, r, :].astype(BF16)
-    for cp in loads[2:]:
-        cp.wait()
     pl.semaphore_wait(barrier, 3)
 
     col_tile = 512
@@ -238,8 +222,8 @@
         later = step > 0
         more = step < n_layers - 1
         end = step == n_layers - 1
-        for cp in w_copies(step):
-            cp.wait()
+        now = w_copies(step)
+        now[0].wait()
 
         @pl.when(more)
         def _():
@@ -259,45 +243,68 @@
 
         @pl.when(later)
         def _():
-            ag_g(3)
+            total = rs_e(3)
+            norm, inv = rms(x2[other])
+            dy2_new = dy2[...] + inv * (total - norm * jnp.mean(total * norm, axis=-1, keepdims=True))
+            dy2[...] = dy2_new
+            ee[rows(me * seq), :] = dy2_new.astype(BF16)
+            ag_f(3)
+        now[1].wait()
         product(0, h_s, w2_s)
         rs_a(0)
 
+        @pl.when(step == 0)
+        def _():
+            loads[1].wait()
+
+            @pl.loop(0, tp)
+            def _(b):
+                r = rows(b * seq)
+                ee[r, :] = part[3, r, :].astype(BF16)
+        rs_b(0)
+
         @pl.when(later)
         def _():
+            ag_g(3)
+        rs_c(0)
+        rs_d(0)
+
+        @pl.when(step == 0)
+        def _():
+            row_id = lax.broadcasted_iota(jnp.int32, (tokens, tokens), 0)
+            col_id = lax.broadcasted_iota(jnp.int32, (tokens, tokens), 1)
+            seen = jnp.zeros((tokens, tokens), F32)
+            for b in range(tp):
+                inside = (row_id < (b + 1) * seq) & (col_id >= b * seq) & (col_id <= row_id) & (col_id < b * seq + lens[b])
+                seen = jnp.where(inside, 1.0, seen)
+            mask[...] = seen
+            for cp in loads[2:]:
+                cp.wait()
+
+        @pl.when(later)
+        def _():
             ag_h(3)
-        rs_b(0)
-
-        @pl.when(later)
-        def _():
             ag_i(3)
         out_copy(2, ee, e_o, layer).start()
-        rs_c(0)
         u_s[...] = (gp[...] * mm(ee[...], w2_s[...], NT)).astype(BF16)
         out_copy(3, u_s, u_o, layer).start()
         product(1, u_s, w1_s)
         rs_a(1)
-        rs_d(0)
         rs_b(1)
-        rs_c(1)
         total = rs_e(0)
         x2_new = x2[other] - total
         x2[slot] = x2_new
         n2[rows(me * seq), :] = rms(x2_new)[0].astype(BF16)
         ag_f(0)
+        rs_c(1)
+        ag_g(0)
         rs_d(1)
-        ag_g(0)
         ag_h(0)
-        total = rs_e(1)
-        norm, inv = rms(x1[other])
-        dy1_new = dy1[...] + inv * (total - norm * jnp.mean(total * norm, axis=-1, keepdims=True))
-        dy1[...] = dy1_new
-        cc[rows(me * seq), :] = dy1_new.astype(BF16)
-        ag_f(1)
+        for cp in now[2:]:
+            cp.wait()
         ag_i(0)
         out_copy(4, n2, n2_o, layer).start()
         qkv[...] = mm(n2[...], wqkv_s[...], NT).astype(BF16)
-        ag_g(1)
         key, val = qkv[:, qw:qw + hd], qkv[:, qw + hd:qw + 2 * hd]
         for r in range(heads):
             sc = mm(qkv[:, r * hd:(r + 1) * hd], key, NT) * scale
@@ -307,25 +314,21 @@
             probs[r] = pr
             att[:, r * hd:(r + 1) * hd] = mm(pr.astype(BF16), val, NN).astype(BF16)
         out_copy(5, att, a_o, layer).start()
-        ag_h(1)
-
-        @pl.when(end)
-        def _():
-            fin_start(1, x2[slot])
+        total = rs_e(1)
+        norm, inv = rms(x1[other])
+        dy1_new = dy1[...] + inv * (total - norm * jnp.mean(total * norm, axis=-1, keepdims=True))
+        dy1[...] = dy1_new
+        cc[rows(me * seq), :] = dy1_new.astype(BF16)
+        ag_f(1)
         product(2, att, wo_s)
         out_copy(0, n1, n1_o, layer).wait()
         rs_a(2)
         rs_b(2)
-
-        @pl.when(end)
-        def _():
-            ag_g(5)
+        ag_g(1)
         rs_c(2)
+        rs_d(2)
+        ag_h(1)
         ag_i(1)
-
-        @pl.when(end)
-        def _():
-            fin_start(2, dy1[...])
         out_copy(6, cc, c_o, layer).start()
         d_att = mm(cc[...], wo_s[...], NT).astype(BF16)
         d_key = jnp.zeros((tokens, hd), F32)
@@ -341,21 +344,15 @@
         dqkv[:, qw:qw + hd] = d_key.astype(BF16)
         dqkv[:, qw + hd:qw + 2 * hd] = d_val.astype(BF16)
         out_copy(7, dqkv, d_o, layer).start()
-        rs_d(2)
-
-        @pl.when(end)
-        def _():
-            ag_h(5)
-            ag_g(6)
         product(3, dqkv, wqkv_s)
         out_copy(2, ee, e_o, layer).wait()
         rs_a(3)
         rs_b(3)
-        rs_c(3)
 
         @pl.when(end)
         def _():
-            ag_h(6)
+            rs_c(3)
+            fin_start(1, x2[slot])
         total = rs_e(2)
         x1_new = x1[other] - total
         x1[slot] = x1_new
@@ -364,36 +361,27 @@
         @pl.when(more)
         def _():
             ag_f(2)
+            rs_c(3)
+            ag_g(2)
+            rs_d(3)
+            ag_h(2)
 
         @pl.when(end)
         def _():
+            rs_d(3)
+            fin_start(2, dy1[...])
             fin_start(0, x1_new)
-        rs_d(3)
-
-        @pl.when(more)
-        def _():
-            ag_g(2)
-            ag_h(2)
-
-        @pl.when(end)
-        def _():
+            ag_g(5)
+            total = rs_e(3)
+            norm, inv = rms(x2[slot])
+            fin_start(3, dy2[...] + inv * (total - norm * jnp.mean(total * norm, axis=-1, keepdims=True)))
+            ag_g(6)
+            ag_h(5)
+            ag_g(4)
+            ag_h(6)
             fin_end(1)
+            ag_h(4)
             fin_end(2)
-            ag_g(4)
-            ag_h(4)
-        total = rs_e(3)
-        norm, inv = rms(x2[slot])
-        dy2_new = dy2[...] + inv * (total - norm * jnp.mean(total * norm, axis=-1, keepdims=True))
-        dy2[...] = dy2_new
-        ee[rows(me * seq), :] = dy2_new.astype(BF16)
-
-        @pl.when(more)
-        def _():
-            ag_f(3)
-
-        @pl.when(end)
-        def _():
-            fin_start(3, dy2_new)
         for k, src, dst in ((1, h_s, h_o), (3, u_s, u_o), (4, n2, n2_o), (5, att, a_o), (6, cc, c_o), (7, dqkv, d_o)):
             out_copy(k, src, dst, layer).wait()
 
@@ -405,8 +393,11 @@
         fin_copy(k).wait()
 
 
-def grad_kernel(parts, n1, n2, c_val, e_val, h_val, u_val, a_val, d_val, g_up, g_down, g_q, g_k, g_v, g_out):
+def grad_kernel(parts, n1, n2, c_val, e_val, h_val, u_val, a_val, d_val, *refs):
     qw, hd = parts
+    ends_in, (g_up, g_down, g_q, g_k, g_v, g_out), ends_out = refs[:4], refs[4:10], refs[10:]
+    for src, dst in zip(ends_in, ends_out):
+        dst[...] = src[...]
     g_up[0] = mm(u_val[0], n1[0], TN)
     g_down[0] = mm(h_val[0], e_val[0], TN)
     g_out[0] = mm(a_val[0], c_val[0], TN)
@@ -473,16 +464,18 @@
             return pl.BlockSpec((1, tokens, cols), lambda layer, j: (layer, 0, 0))
         g_rows = (ff, ff, qw, hd, hd, qw)
         moved = 2 * n_layers * tokens * (4 * width + 2 * ff + 2 * qw + 2 * hd) + 4 * n_layers * width * sum(g_rows)
-        g_up, g_down, g_q, g_k, g_v, g_out = pl.pallas_call(
+        steps = n_layers * (width // col_tile)
+        end_spec = pl.BlockSpec((tokens // steps, width), lambda layer, j: (layer * (width // col_tile) + j, 0))
+        g_up, g_down, g_q, g_k, g_v, g_out, *ends = pl.pallas_call(
             functools.partial(grad_kernel, (qw, hd)),
             grid=(n_layers, width // col_tile),
-            out_shape=tuple(jax.ShapeDtypeStruct((n_layers, r, width), F32) for r in g_rows),
-            in_specs=[wide()] * 4 + [small(ff), small(ff), small(qw), small(qw + 2 * hd)],
-            out_specs=tuple(pl.BlockSpec((1, r, col_tile), lambda layer, j: (layer, 0, j)) for r in g_rows),
+            out_shape=tuple(jax.ShapeDtypeStruct((n_layers, r, width), F32) for r in g_rows) + (jax.ShapeDtypeStruct((tokens, width), F32),) * 4,
+            in_specs=[wide()] * 4 + [small(ff), small(ff), small(qw), small(qw + 2 * hd)] + [end_spec] * 4,
+            out_specs=tuple(pl.BlockSpec((1, r, col_tile), lambda layer, j: (layer, 0, j)) for r in g_rows) + (end_spec,) * 4,
             compiler_params=pltpu.CompilerParams(vmem_limit_bytes=60_000_000),
             cost_estimate=pl.CostEstimate(flops=2 * n_layers * tokens * width * sum(g_rows), bytes_accessed=moved, transcendentals=0),
             name='grads',
-        )(n1, n2, c_val, e_val, h_val, u_val, a_val, d_val)
+        )(n1, n2, c_val, e_val, h_val, u_val, a_val, d_val, *ends)
 
         def flip_back(g, like):
             return g.reshape(n_layers, -1, hd, width).transpose(0, 3, 1, 2).reshape(like.shape)

time: 346 us -> 331 us (0.957)
  local copies, waits for them, and re-layouts: 8.36 us -> 0 us
  Pallas kernels: 336 us -> 330 us
    pallas_call x1, Pallas kernels: 306 us -> 295 us  [local_fn(): pl.pallas_call(functools.partial(chain_kernel, (n_layers, tp, seq, width,...]
    unnamed x12 -> x0, local copies, waits for them, and re-layouts: 8.36 us -> none
    pallas_call x1, Pallas kernels: 30.1 us -> 35.2 us  [local_fn(): pl.pallas_call(functools.partial(grad_kernel, (qw, hd)), grid=(n_layers,...]
where the time goes in v3:
time: 331 us; the launch traced here: 330 us
  Pallas kernels  330 us (100%)
    pallas_call x1, Pallas kernels, local_fn(): pl.pallas_call(functools.partial(chain_kernel, (n_layers, tp, seq, width,...  295 us
    pallas_call x1, Pallas kernels, local_fn(): pl.pallas_call(functools.partial(grad_kernel, (qw, hd)), grid=(n_layers,...  35.2 us

profile of v3, /device:TPU:113, one launch (start us, length us, event | category | flops | bytes accessed | tf_op | source)
XLA Modules:
  0.0 330.5 jit_solution(15880686747865440683)
XLA Ops:
  0.6 294.7 %chain.1 = (f32[256,2048]{1,0:T(8,128)}, f32[256,2048]{1,0:T(8,128)}, f32[256,2048]{1,0:T(8,128)}, f32[256,2048]{1,0:T(8,128)}, bf16[4,256,2048]{2,1,0:T(8,128)(...) custom-call(s32[8]{0:T(128)} %lens.1, ...), custom_call_target="tpu_custom_call" | custom-call | tf_op jit(solution)/shard_map/chain/pallas_call | solution.py:447
  295.3 35.2 %grads.1 = (f32[4,704,2048]{2,1,0:T(8,128)}, f32[4,704,2048]{2,1,0:T(8,128)}, f32[4,256,2048]{2,1,0:T(8,128)}, f32[4,64,2048]{2,1,0:T(8,128)}, f32[4,64,2048]{2,...) custom-call(bf16[4,256,2048]{2,1,0:T(8,128)(2,1)} %get-tuple-element, ...), custom_call_target="tpu_custom_call" | custom-call | flops 8589934592 | bytes 88080384 | tf_op jit(solution)/shard_map/grads/pallas_call | solution.py:469

commit v4 on v3

v4 whole, which is shorter than its diff:
```python
import functools

import jax
import jax.numpy as jnp
from jax import lax
from jax.experimental import pallas as pl
from jax.experimental.pallas import tpu as pltpu
from jax.sharding import PartitionSpec as P

F32 = jnp.float32
BF16 = jnp.bfloat16
EPS = 1e-5
MASK_VALUE = -1e30
GELU_C = 0.7978845608028654
GELU_A = 0.044715
MESH = pl.DeviceIdType.MESH
NT = (((1,), (1,)), ((), ()))
NN = (((1,), (0,)), ((), ()))
TN = (((0,), (0,)), ((), ()))


def mm(lhs, rhs, dims):
    return lax.dot_general(lhs, rhs, dims, preferred_element_type=F32)


def chain_kernel(cfg, lens, y1_h, y2_h, dy1_h, dy2_h, w1_h, w2_h, wq_h, wk_h, wv_h, wo_h,
                 f_x1, f_x2, f_dy1, f_dy2, n1_o, n2_o, c_o, e_o, h_o, u_o, a_o, d_o,
                 n1, n2, cc, ee, w1, w2, wqkv, wo, h_s, u_s, gp, qkv, att, dqkv, probs, mask,
                 x1, x2, dy1, dy2, part, ra, rb, rc, fbuf,
                 w_sem, in_sem, out_sem, fin_sem, rs_send, rs_recv, ag_send, ag_recv):
    n_layers, tp, seq, width, heads, hd = cfg
    chips = tp // 2
    tokens = tp * seq
    ht = tokens // 2
    own = ht // tp
    hw = width // 2
    scale = hd ** -0.5
    qw = heads * hd
    me = lax.axis_index('tp')
    chip = me // 2
    core = me - 2 * chip
    partner = me + 1 - 2 * core
    right = lax.rem(me + 2, tp)
    left = lax.rem(me + tp - 2, tp)
    opp = lax.rem(me + chips, tp)
    lo, hi, every = pl.ds(0, hw), pl.ds(hw, hw), pl.ds(0, width)
    halves = (pl.ds(0, ht), pl.ds(ht, ht))

    def rows(hb, who):
        return pl.ds(pl.multiple_of(hb * ht + who * own, own), own)

    def rcopy(src, dst, send, recv, dev):
        return pltpu.make_async_remote_copy(src_ref=src, dst_ref=dst, send_sem=send, recv_sem=recv,
                                            device_id={'tp': dev}, device_id_type=MESH)

    def w_copies(step):
        layer = n_layers - 1 - step
        slot = lax.rem(step, 2)
        kw = wk_h.shape[1]
        return (pltpu.make_async_copy(w1_h.at[layer], w1.at[slot], w_sem.at[slot, 0]),
                pltpu.make_async_copy(w2_h.at[layer], w2.at[slot], w_sem.at[slot, 1]),
                pltpu.make_async_copy(wq_h.at[layer], wqkv.at[slot, pl.ds(0, qw)], w_sem.at[slot, 2]),
                pltpu.make_async_copy(wk_h.at[layer], wqkv.at[slot, pl.ds(qw, kw)], w_sem.at[slot, 3]),
                pltpu.make_async_copy(wv_h.at[layer], wqkv.at[slot, pl.ds(qw + kw, kw)], w_sem.at[slot, 4]),
                pltpu.make_async_copy(wo_h.at[layer], wo.at[slot], w_sem.at[slot, 5]))

    owners = (opp, right, left, me)

    def rs_d2d(i, role):
        theirs = owners[role] + 1 - 2 * core
        return rcopy(part.at[i, rows(0, theirs)], ra.at[i, role], rs_send.at[i, role], rs_recv.at[i, role], partner)

    def rs_ring(i, kind):
        who, cols, dst, dev = ((opp, lo, rb.at[i, 0], right), (opp, hi, rb.at[i, 1], left),
                               (right, hi, rc.at[i, 0, :, hi], right), (left, lo, rc.at[i, 1, :, lo], left),
                               (right, lo, rc.at[i, 0, :, lo], right), (left, hi, rc.at[i, 1, :, hi], left))[kind]
        return rcopy(part.at[i, rows(0, who), cols], dst, rs_send.at[i, 4 + kind], rs_recv.at[i, 4 + kind], dev)

    def rs_add(i, who, cols, extra):
        r = rows(0, who)
        part[i, r, cols] = part[i, r, cols] + extra

    def rs_a(i):
        for role in range(4):
            rs_d2d(i, role).start()

    def rs_b(i):
        rs_d2d(i, 0).wait_recv()
        rs_add(i, opp, every, ra[i, 0])
        rs_ring(i, 0).start()
        rs_ring(i, 1).start()

    def rs_c(i):
        rs_d2d(i, 1).wait_recv()
        rs_add(i, right, every, ra[i, 1])
        rs_ring(i, 2).start()
        rs_d2d(i, 2).wait_recv()
        rs_add(i, left, every, ra[i, 2])
        rs_ring(i, 3).start()

    def rs_d(i):
        rs_ring(i, 0).wait_recv()
        rs_add(i, right, lo, rb[i, 0])
        rs_ring(i, 4).start()
        rs_ring(i, 1).wait_recv()
        rs_add(i, left, hi, rb[i, 1])
        rs_ring(i, 5).start()

    def rs_e(i):
        rs_d2d(i, 3).wait_recv()
        for kind in range(2, 6):
            rs_ring(i, kind).wait_recv()
        for role in range(4):
            rs_d2d(i, role).wait_send()
        for kind in range(6):
            rs_ring(i, kind).wait_send()
        return (part[i, rows(0, me), :] + ra[i, 3]) + (rc[i, 0] + rc[i, 1])

    bufs = (n2, n2, cc, cc, n1, n1, ee, ee)
    f_pos = (1, 1, 2, 2, 0, 0, 3, 3)
    f_out = (f_x1, f_x2, f_dy1, f_dy2)

    def ag_msg(i, kind, fin, receive=False):
        buf = fbuf.at[f_pos[i]] if fin else bufs[i]
        if receive:
            whos = (left, right, partner, opp, opp, lax.rem(partner + tp - 2, tp), lax.rem(partner + 2, tp),
                    lax.rem(partner + chips, tp), lax.rem(partner + chips, tp))
        else:
            whos = (me, me, me, left, right, left, right, opp, opp)
        cols = (every, every, every, lo, hi, every, every, lo, hi)[kind]
        dev = (right, left, partner, right, left, partner, partner, partner, partner)[kind]
        ref = buf.at[rows(i % 2, whos[kind]), cols]
        return rcopy(ref, ref, ag_send.at[i, kind], ag_recv.at[i, kind], dev)

    def ag_f(i, fin=False):
        for kind in range(3):
            ag_msg(i, kind, fin).start()

    def ag_g(i, fin=False):
        ag_msg(i, 0, fin, True).wait_recv()
        ag_msg(i, 3, fin).start()
        ag_msg(i, 5, fin).start()
        ag_msg(i, 1, fin, True).wait_recv()
        ag_msg(i, 4, fin).start()
        ag_msg(i, 6, fin).start()

    def ag_h(i, fin=False):
        ag_msg(i, 3, fin, True).wait_recv()
        ag_msg(i, 7, fin).start()
        ag_msg(i, 4, fin, True).wait_recv()
        ag_msg(i, 8, fin).start()

    def fin_copy(i):
        r = halves[i % 2]
        return pltpu.make_async_copy(fbuf.at[f_pos[i], r], f_out[f_pos[i]].at[r], fin_sem.at[i])

    def ag_i(i, fin=False):
        for kind in (2, 5, 6, 7, 8):
            ag_msg(i, kind, fin, True).wait_recv()
        for kind in range(9):
            ag_msg(i, kind, fin).wait_send()
        if fin:
            fin_copy(i).start()

    def fin_start(i, value):
        fbuf[f_pos[i], rows(i % 2, me), :] = value
        ag_f(i, True)

    def out_copy(k, hb, src, dst, layer):
        r = halves[hb]
        return pltpu.make_async_copy(src.at[r], dst.at[layer, r], out_sem.at[k, hb])

    def rms(x_val):
        inv = lax.rsqrt(jnp.mean(x_val * x_val, axis=-1, keepdims=True) + EPS)
        return x_val * inv, inv

    def rms_back(x_val, grad):
        norm, inv = rms(x_val)
        return inv * (grad - norm * jnp.mean(grad * norm, axis=-1, keepdims=True))

    barrier = pltpu.get_barrier_semaphore()
    for other in (partner, right, left):
        pl.semaphore_signal(barrier, inc=1, device_id={'tp': other}, device_id_type=MESH)
    y_loads = [pltpu.make_async_copy(y1_h.at[halves[hb]], part.at[4 + hb], in_sem.at[hb]) for hb in range(2)]
    d_loads = [pltpu.make_async_copy(dy2_h.at[halves[hb]], part.at[6 + hb], in_sem.at[2 + hb]) for hb in range(2)]
    loads = []
    for hb in range(2):
        r = rows(hb, me)
        for k, (src, dst) in enumerate(((y1_h, x1.at[1, hb]), (y2_h, x2.at[1, hb]), (dy1_h, dy1.at[hb]), (dy2_h, dy2.at[hb]))):
            loads.append(pltpu.make_async_copy(src.at[r], dst, in_sem.at[4 + 4 * hb + k]))
    first = w_copies(0)
    for cp in (y_loads[0], first[0], y_loads[1], first[1], *d_loads, *loads, *first[2:]):
        cp.start()
    chunk = 32
    for hb in range(2):
        y_loads[hb].wait()

        @pl.loop(0, ht // chunk)
        def _(b):
            src = pl.ds(pl.multiple_of(b * chunk, chunk), chunk)
            n1[pl.ds(pl.multiple_of(hb * ht + b * chunk, chunk), chunk), :] = rms(part[4 + hb, src, :])[0].astype(BF16)
    pl.semaphore_wait(barrier, 3)

    col_tile = 512

    def product(i, lhs_ref, w_ref):
        @pl.loop(0, width // col_tile)
        def _(j):
            cols = pl.ds(pl.multiple_of(j * col_tile, col_tile), col_tile)
            part[i, :, cols] = mm(lhs_ref[halves[i % 2], :], w_ref[:, cols], NN)

    def finish(i, slot, fin):
        hb = i % 2
        mine = rows(hb, me)
        total = rs_e(i)
        if i < 2:
            new = x2[1 - slot, hb] - total
            x2[slot, hb] = new
            n2[mine, :] = rms(new)[0].astype(BF16)
        elif i < 4:
            new = dy1[hb] + rms_back(x1[1 - slot, hb], total)
            dy1[hb] = new
            cc[mine, :] = new.astype(BF16)
        elif i < 6:
            new = x1[1 - slot, hb] - total
            x1[slot, hb] = new
            n1[mine, :] = rms(new)[0].astype(BF16)
        else:
            new = dy2[hb] + rms_back(x2[slot, hb], total)
            dy2[hb] = new
            ee[mine, :] = new.astype(BF16)
        if fin is True:
            fin_start(i, new)
        elif fin is False:
            ag_f(i)
        else:
            pl.when(fin)(lambda: fin_start(i, new))
            pl.when(jnp.logical_not(fin))(lambda: ag_f(i))

    def either(fn, i, end):
        if i < 4:
            fn(i)
        else:
            pl.when(end)(lambda: fn(i, True))
            pl.when(jnp.logical_not(end))(lambda: fn(i))

    @pl.loop(0, n_layers)
    def _(step):
        layer = n_layers - 1 - step
        slot = lax.rem(step, 2)
        w1_s, w2_s, wqkv_s, wo_s = w1.at[slot], w2.at[slot], wqkv.at[slot], wo.at[slot]
        later = step > 0
        more = step < n_layers - 1
        end = step == n_layers - 1
        now = w_copies(step)

        def compute(i):
            hb = i % 2
            r = halves[hb]
            if i == 0:
                now[0].wait()

                @pl.when(more)
                def _():
                    for cp in w_copies(step + 1):
                        cp.start()
            if i < 2:
                out_copy(0, hb, n1, n1_o, layer).start()
                pre = mm(n1[r, :], w1_s[...], NT)
                tan = jnp.tanh(GELU_C * (pre + GELU_A * (pre * pre * pre)))
                cdf = 0.5 * (1.0 + tan)
                h_s[r, :] = (pre * cdf).astype(BF16)
                gp[r, :] = cdf + pre * (0.5 * GELU_C) * (1.0 - tan * tan) * (1.0 + (3.0 * GELU_A) * (pre * pre))
                out_copy(1, hb, h_s, h_o, layer).start()
            elif i < 4:
                out_copy(2, hb, ee, e_o, layer).start()
                u_s[r, :] = (gp[r, :] * mm(ee[r, :], w2_s[...], NT)).astype(BF16)
                out_copy(3, hb, u_s, u_o, layer).start()
            elif i < 6:
                if i == 4:
                    for cp in now[2:]:
                        cp.wait()
                out_copy(4, hb, n2, n2_o, layer).start()
                qkv[r, :] = mm(n2[r, :], wqkv_s[...], NT).astype(BF16)
                key, val = qkv[r, qw:qw + hd], qkv[r, qw + hd:qw + 2 * hd]
                seen = mask[hb] > 0.5
                for head in range(heads):
                    cols = pl.ds(head * hd, hd)
                    sc = jnp.where(seen, mm(qkv[r, cols], key, NT) * scale, MASK_VALUE)
                    ex = jnp.exp(sc - jnp.max(sc, axis=-1, keepdims=True))
                    pr = ex / jnp.sum(ex, axis=-1, keepdims=True)
                    probs[head, r, :] = pr
                    att[r, cols] = mm(pr.astype(BF16), val, NN).astype(BF16)
                out_copy(5, hb, att, a_o, layer).start()
            else:
                out_copy(6, hb, cc, c_o, layer).start()
                d_att = mm(cc[r, :], wo_s[...], NT).astype(BF16)
                key, val = qkv[r, qw:qw + hd], qkv[r, qw + hd:qw + 2 * hd]
                d_key = jnp.zeros((ht, hd), F32)
                d_val = jnp.zeros((ht, hd), F32)
                for head in range(heads):
                    cols = pl.ds(head * hd, hd)
                    da = d_att[:, head * hd:(head + 1) * hd]
                    pr = probs[head, r, :]
                    dp = mm(da, val, NT)
                    ds = (pr * (dp - jnp.sum(dp * pr, axis=-1, keepdims=True)) * scale).astype(BF16)
                    dqkv[r, cols] = mm(ds, key, NN).astype(BF16)
                    d_key = d_key + mm(ds, qkv[r, cols], TN)
                    d_val = d_val + mm(pr.astype(BF16), da, TN)
                dqkv[r, qw:qw + hd] = d_key.astype(BF16)
                dqkv[r, qw + hd:qw + 2 * hd] = d_val.astype(BF16)
                out_copy(7, hb, dqkv, d_o, layer).start()

        def send(i):
            hb = i % 2
            if i == 0:
                now[1].wait()
            product(i, (h_s, u_s, att, dqkv)[i // 2], (w2_s, w1_s, wo_s, wqkv_s)[i // 2])
            if 4 <= i < 6:
                out_copy(0, hb, n1, n1_o, layer).wait()
            if i >= 6:
                out_copy(2, hb, ee, e_o, layer).wait()
            rs_a(i)

        def guarded(fn, i, back):
            w = (i - back) % 8
            if i < back:
                pl.when(later)(lambda: fn(w))
            elif fn is rs_d:
                fn(w)
            else:
                either(fn, w, end)

        for i in range(8):
            if i < 2:
                pl.when(later)(lambda: finish((i - 2) % 8, 1 - slot, False))
            else:
                finish(i - 2, slot, end if i >= 6 else False)
            compute(i)
            guarded(rs_d, i, 1)
            guarded(ag_h, i, 3)
            send(i)
            rs_b(i)
            guarded(ag_g, i, 2)
            rs_c(i)
            guarded(ag_i, i, 3)
            if i == 0:
                @pl.when(step == 0)
                def _():
                    for hb in range(2):
                        d_loads[hb].wait()

                        @pl.loop(0, ht // chunk)
                        def _(b):
                            src = pl.ds(pl.multiple_of(b * chunk, chunk), chunk)
                            ee[pl.ds(pl.multiple_of(hb * ht + b * chunk, chunk), chunk), :] = part[6 + hb, src, :].astype(BF16)
                        row_id = lax.broadcasted_iota(jnp.int32, (ht, ht), 0)
                        col_id = lax.broadcasted_iota(jnp.int32, (ht, ht), 1)
                        seen = jnp.zeros((ht, ht), F32)
                        for b in range(ht // seq):
                            inside = ((row_id < (b + 1) * seq) & (col_id >= b * seq) & (col_id <= row_id)
                                      & (col_id < b * seq + lens[hb * (ht // seq) + b]))
                            seen = jnp.where(inside, 1.0, seen)
                        mask[hb] = seen
                    for cp in loads:
                        cp.wait()
            if i == 6:
                @pl.when(end)
                def _():
                    fin_start(0, x2[slot, 0])
                    fin_start(1, x2[slot, 1])
            if i == 7:
                @pl.when(end)
                def _():
                    ag_g(0, True)
                    ag_g(1, True)
        for hb in range(2):
            for k, src, dst in ((1, h_s, h_o), (3, u_s, u_o), (4, n2, n2_o), (5, att, a_o), (6, cc, c_o), (7, dqkv, d_o)):
                out_copy(k, hb, src, dst, layer).wait()

    last = (n_layers - 1) % 2
    rs_d(7)
    finish(6, last, True)
    fin_start(2, dy1[0])
    ag_h(5, True)
    ag_h(0, True)
    ag_h(1, True)
    finish(7, last, True)
    fin_start(3, dy1[1])
    for i in (6, 2, 7, 3):
        ag_g(i, True)
    for i in (5, 0, 1):
        ag_i(i, True)
    for i in (6, 2, 7, 3):
        ag_h(i, True)
    for i in (6, 2, 7, 3):
        ag_i(i, True)
    for i in range(8):
        fin_copy(i).wait()


def grad_kernel(parts, n1, n2, c_val, e_val, h_val, u_val, a_val, d_val, *refs):
    qw, hd = parts
    ends_in, (g_up, g_down, g_q, g_k, g_v, g_out), ends_out = refs[:4], refs[4:10], refs[10:]
    for src, dst in zip(ends_in, ends_out):
        dst[...] = src[...]
    g_up[0] = mm(u_val[0], n1[0], TN)
    g_down[0] = mm(h_val[0], e_val[0], TN)
    g_out[0] = mm(a_val[0], c_val[0], TN)
    g_all = mm(d_val[0], n2[0], TN)
    g_q[0] = g_all[:qw]
    g_k[0] = g_all[qw:qw + hd]
    g_v[0] = g_all[qw + hd:]


def solution(mesh):
    tp = mesh.shape['tp']
    assert tp == 8
    act_spec = P('dp', None, None)
    w_specs = (P(None, None, 'tp', None), P(None, None, 'tp', None), P(None, None, 'tp', None),
               P(None, 'tp', None, None), P(None, None, 'tp'), P(None, 'tp', None))
    g_specs = (P('dp', None, 'tp', None), P('dp', None, 'tp', None), P('dp', None, 'tp', None),
               P('dp', 'tp', None, None), P('dp', None, 'tp'), P('dp', 'tp', None))

    def local_fn(y_one, y_two, dy_one, dy_two, seq_lens, w_query, w_key, w_value, w_out, w_up, w_down):
        batch, seq, width = y_one.shape
        n_layers, _, heads, hd = w_query.shape
        assert batch == tp and w_key.shape[2] == 1
        tokens = batch * seq
        ff = w_down.shape[1]
        qw = heads * hd
        ht = tokens // 2
        own = ht // tp
        assert ht % seq == 0 and own % 16 == 0
        acts = [x.reshape(tokens, width) for x in (y_one, y_two, dy_one, dy_two)]

        def flip(w):
            return w.transpose(0, 2, 3, 1).reshape(n_layers, -1, width)
        weights = (w_up.transpose(0, 2, 1), w_down, flip(w_query), flip(w_key), flip(w_value), w_out.reshape(n_layers, qw, width))

        def stack(cols):
            return jax.ShapeDtypeStruct((n_layers, tokens, cols), BF16)
        any_spec = pl.BlockSpec(memory_space=pl.ANY)
        vm = pltpu.VMEM
        dma = pltpu.SemaphoreType.DMA
        scratch = [vm((tokens, width), BF16)] * 4 + [
            vm((2, ff, width), BF16), vm((2, ff, width), BF16), vm((2, qw + 2 * hd, width), BF16), vm((2, qw, width), BF16),
            vm((tokens, ff), BF16), vm((tokens, ff), BF16), vm((tokens, ff), F32),
            vm((tokens, qw + 2 * hd), BF16), vm((tokens, qw), BF16), vm((tokens, qw + 2 * hd), BF16),
            vm((heads, tokens, ht), F32), vm((2, ht, ht), F32),
            vm((2, 2, own, width), F32), vm((2, 2, own, width), F32), vm((2, own, width), F32), vm((2, own, width), F32),
            vm((8, ht, width), F32), vm((8, 4, own, width), F32), vm((8, 2, own, width // 2), F32), vm((8, 2, own, width), F32),
            vm((4, tokens, width), F32),
            dma((2, 6)), dma((12,)), dma((8, 2)), dma((8,)), dma((8, 10)), dma((8, 10)), dma((8, 9)), dma((8, 9))]
        *ends, n1, n2, c_val, e_val, h_val, u_val, a_val, d_val = pl.pallas_call(
            functools.partial(chain_kernel, (n_layers, tp, seq, width, heads, hd)),
            out_shape=(jax.ShapeDtypeStruct((tokens, width), F32),) * 4 + (stack(width), stack(width), stack(width), stack(width),
                       stack(ff), stack(ff), stack(qw), stack(qw + 2 * hd)),
            in_specs=[pl.BlockSpec(memory_space=pltpu.SMEM)] + [any_spec] * 10,
            out_specs=(any_spec,) * 12,
            scratch_shapes=scratch,
            compiler_params=pltpu.CompilerParams(collective_id=0, has_side_effects=True, vmem_limit_bytes=66_000_000),
            name='chain',
        )(seq_lens, *acts, *weights)

        col_tile = 512

        def wide():
            return pl.BlockSpec((1, tokens, col_tile), lambda layer, j: (layer, 0, j))

        def small(cols):
            return pl.BlockSpec((1, tokens, cols), lambda layer, j: (layer, 0, 0))
        g_rows = (ff, ff, qw, hd, hd, qw)
        moved = 2 * n_layers * tokens * (4 * width + 2 * ff + 2 * qw + 2 * hd) + 4 * n_layers * width * sum(g_rows)
        steps = n_layers * (width // col_tile)
        end_spec = pl.BlockSpec((tokens // steps, width), lambda layer, j: (layer * (width // col_tile) + j, 0))
        g_up, g_down, g_q, g_k, g_v, g_out, *ends = pl.pallas_call(
            functools.partial(grad_kernel, (qw, hd)),
            grid=(n_layers, width // col_tile),
            out_shape=tuple(jax.ShapeDtypeStruct((n_layers, r, width), F32) for r in g_rows) + (jax.ShapeDtypeStruct((tokens, width), F32),) * 4,
            in_specs=[wide()] * 4 + [small(ff), small(ff), small(qw), small(qw + 2 * hd)] + [end_spec] * 4,
            out_specs=tuple(pl.BlockSpec((1, r, col_tile), lambda layer, j: (layer, 0, j)) for r in g_rows) + (end_spec,) * 4,
            compiler_params=pltpu.CompilerParams(vmem_limit_bytes=60_000_000),
            cost_estimate=pl.CostEstimate(flops=2 * n_layers * tokens * width * sum(g_rows), bytes_accessed=moved, transcendentals=0),
            name='grads',
        )(n1, n2, c_val, e_val, h_val, u_val, a_val, d_val, *ends)

        def flip_back(g, like):
            return g.reshape(n_layers, -1, hd, width).transpose(0, 3, 1, 2).reshape(like.shape)
        dw_up, dw_down, dw_out = g_up.transpose(0, 2, 1), g_down, g_out.reshape(w_out.shape)
        dw_query, dw_key, dw_value = flip_back(g_q, w_query), flip_back(g_k, w_key), flip_back(g_v, w_value)
        ends = tuple(v.reshape(batch, seq, width) for v in ends)
        return ends + (dw_query, dw_key, dw_value, dw_out, dw_up, dw_down)

    return jax.shard_map(local_fn, mesh=mesh,
                         in_specs=(act_spec,) * 4 + (P('dp'),) + w_specs,
                         out_specs=(act_spec,) * 4 + g_specs,
                         check_vma=False)
```

time: 331 us -> 302 us (0.912)
  Pallas kernels: 330 us -> 300 us
    pallas_call x1, Pallas kernels: 295 us -> 265 us  [local_fn(): pl.pallas_call(functools.partial(chain_kernel, (n_layers, tp, seq, width,...]
where the time goes in v4:
time: 302 us; the launch traced here: 301 us
  Pallas kernels  300 us (99%)
    pallas_call x1, Pallas kernels, local_fn(): pl.pallas_call(functools.partial(chain_kernel, (n_layers, tp, seq, width,...  265 us
    pallas_call x1, Pallas kernels, local_fn(): pl.pallas_call(functools.partial(grad_kernel, (qw, hd)), grid=(n_layers,...  35.2 us

profile of v4, /device:TPU:113, one launch (start us, length us, event | category | flops | bytes accessed | tf_op | source)
XLA Modules:
  0.0 301.3 jit_solution(7759343190302834540)
XLA Ops:
  0.6 265.3 %chain.1 = (f32[256,2048]{1,0:T(8,128)}, f32[256,2048]{1,0:T(8,128)}, f32[256,2048]{1,0:T(8,128)}, f32[256,2048]{1,0:T(8,128)}, bf16[4,256,2048]{2,1,0:T(8,128)(...) custom-call(s32[8]{0:T(128)} %lens.1, ...), custom_call_target="tpu_custom_call" | custom-call | tf_op jit(solution)/shard_map/chain/pallas_call | solution.py:455
  266.0 35.2 %grads.1 = (f32[4,704,2048]{2,1,0:T(8,128)}, f32[4,704,2048]{2,1,0:T(8,128)}, f32[4,256,2048]{2,1,0:T(8,128)}, f32[4,64,2048]{2,1,0:T(8,128)}, f32[4,64,2048]{2,...) custom-call(bf16[4,256,2048]{2,1,0:T(8,128)(2,1)} %get-tuple-element, ...), custom_call_target="tpu_custom_call" | custom-call | flops 8589934592 | bytes 88080384 | tf_op jit(solution)/shard_map/grads/pallas_call | solution.py:477

commit v5 on v4

--- a/solution.py
+++ b/solution.py
@@ -34,6 +34,7 @@
     ht = tokens // 2
     own = ht // tp
     hw = width // 2
+    chunk = 32
     scale = hd ** -0.5
     qw = heads * hd
     me = lax.axis_index('tp')
@@ -161,6 +162,12 @@
             ag_msg(i, kind, fin).wait_send()
         if fin:
             fin_copy(i).start()
+        if fin and i < 4:
+            @pl.loop(0, ht // chunk)
+            def _(b):
+                r = pl.ds(pl.multiple_of((i % 2) * ht + b * chunk, chunk), chunk)
+                got = fbuf[f_pos[i], r, :]
+                bufs[i][r, :] = (rms(got)[0] if i < 2 else got).astype(BF16)
 
     def fin_start(i, value):
         fbuf[f_pos[i], rows(i % 2, me), :] = value
@@ -189,16 +196,18 @@
         for k, (src, dst) in enumerate(((y1_h, x1.at[1, hb]), (y2_h, x2.at[1, hb]), (dy1_h, dy1.at[hb]), (dy2_h, dy2.at[hb]))):
             loads.append(pltpu.make_async_copy(src.at[r], dst, in_sem.at[4 + 4 * hb + k]))
     first = w_copies(0)
-    for cp in (y_loads[0], first[0], y_loads[1], first[1], *d_loads, *loads, *first[2:]):
+    y_loads[0].start()
+    first[0].start()
+    y_loads[0].wait()
+    for cp in (first[1], y_loads[1], *d_loads, *loads, *first[2:]):
         cp.start()
-    chunk = 32
-    for hb in range(2):
-        y_loads[hb].wait()
-
+
+    def rounded(dst, i, fn):
         @pl.loop(0, ht // chunk)
         def _(b):
             src = pl.ds(pl.multiple_of(b * chunk, chunk), chunk)
-            n1[pl.ds(pl.multiple_of(hb * ht + b * chunk, chunk), chunk), :] = rms(part[4 + hb, src, :])[0].astype(BF16)
+            dst[pl.ds(pl.multiple_of((i % 2) * ht + b * chunk, chunk), chunk), :] = fn(part[i, src, :]).astype(BF16)
+    rounded(n1, 4, lambda x: rms(x)[0])
     pl.semaphore_wait(barrier, 3)
 
     col_tile = 512
@@ -216,33 +225,30 @@
         if i < 2:
             new = x2[1 - slot, hb] - total
             x2[slot, hb] = new
-            n2[mine, :] = rms(new)[0].astype(BF16)
         elif i < 4:
             new = dy1[hb] + rms_back(x1[1 - slot, hb], total)
             dy1[hb] = new
-            cc[mine, :] = new.astype(BF16)
         elif i < 6:
             new = x1[1 - slot, hb] - total
             x1[slot, hb] = new
-            n1[mine, :] = rms(new)[0].astype(BF16)
         else:
             new = dy2[hb] + rms_back(x2[slot, hb], total)
             dy2[hb] = new
-            ee[mine, :] = new.astype(BF16)
+
+        def send_b():
+            bufs[i][mine, :] = (rms(new)[0] if i in (0, 1, 4, 5) else new).astype(BF16)
+            ag_f(i)
         if fin is True:
             fin_start(i, new)
         elif fin is False:
-            ag_f(i)
+            send_b()
         else:
             pl.when(fin)(lambda: fin_start(i, new))
-            pl.when(jnp.logical_not(fin))(lambda: ag_f(i))
+            pl.when(jnp.logical_not(fin))(send_b)
 
     def either(fn, i, end):
-        if i < 4:
-            fn(i)
-        else:
-            pl.when(end)(lambda: fn(i, True))
-            pl.when(jnp.logical_not(end))(lambda: fn(i))
+        pl.when(end)(lambda: fn(i, True))
+        pl.when(jnp.logical_not(end))(lambda: fn(i))
 
     @pl.loop(0, n_layers)
     def _(step):
@@ -335,25 +341,26 @@
             if i < 2:
                 pl.when(later)(lambda: finish((i - 2) % 8, 1 - slot, False))
             else:
-                finish(i - 2, slot, end if i >= 6 else False)
+                finish(i - 2, slot, end)
             compute(i)
             guarded(rs_d, i, 1)
             guarded(ag_h, i, 3)
             send(i)
+            if i == 0:
+                @pl.when(step == 0)
+                def _():
+                    y_loads[1].wait()
+                    rounded(n1, 5, lambda x: rms(x)[0])
             rs_b(i)
             guarded(ag_g, i, 2)
             rs_c(i)
             guarded(ag_i, i, 3)
-            if i == 0:
+            if i == 1:
                 @pl.when(step == 0)
                 def _():
                     for hb in range(2):
                         d_loads[hb].wait()
-
-                        @pl.loop(0, ht // chunk)
-                        def _(b):
-                            src = pl.ds(pl.multiple_of(b * chunk, chunk), chunk)
-                            ee[pl.ds(pl.multiple_of(hb * ht + b * chunk, chunk), chunk), :] = part[6 + hb, src, :].astype(BF16)
+                        rounded(ee, 6 + hb, lambda x: x)
                         row_id = lax.broadcasted_iota(jnp.int32, (ht, ht), 0)
                         col_id = lax.broadcasted_iota(jnp.int32, (ht, ht), 1)
                         seen = jnp.zeros((ht, ht), F32)
@@ -364,16 +371,6 @@
                         mask[hb] = seen
                     for cp in loads:
                         cp.wait()
-            if i == 6:
-                @pl.when(end)
-                def _():
-                    fin_start(0, x2[slot, 0])
-                    fin_start(1, x2[slot, 1])
-            if i == 7:
-                @pl.when(end)
-                def _():
-                    ag_g(0, True)
-                    ag_g(1, True)
         for hb in range(2):
             for k, src, dst in ((1, h_s, h_o), (3, u_s, u_o), (4, n2, n2_o), (5, att, a_o), (6, cc, c_o), (7, dqkv, d_o)):
                 out_copy(k, hb, src, dst, layer).wait()
@@ -381,19 +378,14 @@
     last = (n_layers - 1) % 2
     rs_d(7)
     finish(6, last, True)
-    fin_start(2, dy1[0])
     ag_h(5, True)
-    ag_h(0, True)
-    ag_h(1, True)
     finish(7, last, True)
-    fin_start(3, dy1[1])
-    for i in (6, 2, 7, 3):
+    ag_i(5, True)
+    for i in (6, 7):
         ag_g(i, True)
-    for i in (5, 0, 1):
-        ag_i(i, True)
-    for i in (6, 2, 7, 3):
+    for i in (6, 7):
         ag_h(i, True)
-    for i in (6, 2, 7, 3):
+    for i in (6, 7):
         ag_i(i, True)
     for i in range(8):
         fin_copy(i).wait()

time: 302 us -> 292 us (0.967)
  Pallas kernels: 300 us -> 291 us
    pallas_call x1, Pallas kernels: 265 us -> 256 us  [local_fn(): pl.pallas_call(functools.partial(chain_kernel, (n_layers, tp, seq, width,...]
where the time goes in v5:
time: 292 us
  Pallas kernels  291 us (100%)
    pallas_call x1, Pallas kernels, local_fn(): pl.pallas_call(functools.partial(chain_kernel, (n_layers, tp, seq, width,...  256 us
    pallas_call x1, Pallas kernels, local_fn(): pl.pallas_call(functools.partial(grad_kernel, (qw, hd)), grid=(n_layers,...  35.2 us

profile of v5, /device:TPU:113, one launch (start us, length us, event | category | flops | bytes accessed | tf_op | source)
XLA Modules:
  0.0 291.5 jit_solution(15428383201122753751)
XLA Ops:
  0.6 255.7 %chain.1 = (f32[256,2048]{1,0:T(8,128)}, f32[256,2048]{1,0:T(8,128)}, f32[256,2048]{1,0:T(8,128)}, f32[256,2048]{1,0:T(8,128)}, bf16[4,256,2048]{2,1,0:T(8,128)(...) custom-call(s32[8]{0:T(128)} %lens.1, ...), custom_call_target="tpu_custom_call" | custom-call | tf_op jit(solution)/shard_map/chain/pallas_call | solution.py:447
  256.3 35.2 %grads.1 = (f32[4,704,2048]{2,1,0:T(8,128)}, f32[4,704,2048]{2,1,0:T(8,128)}, f32[4,256,2048]{2,1,0:T(8,128)}, f32[4,64,2048]{2,1,0:T(8,128)}, f32[4,64,2048]{2,...) custom-call(bf16[4,256,2048]{2,1,0:T(8,128)(2,1)} %get-tuple-element, ...), custom_call_target="tpu_custom_call" | custom-call | flops 8589934592 | bytes 88080384 | tf_op jit(solution)/shard_map/grads/pallas_call | solution.py:469

commit v6 on v5

--- a/solution.py
+++ b/solution.py
@@ -81,15 +81,24 @@
         r = rows(0, who)
         part[i, r, cols] = part[i, r, cols] + extra
 
+    n_tiles = 4
+    tiles = [pl.ds(t * (width // n_tiles), width // n_tiles) for t in range(n_tiles)]
+
+    def rs_first(i, t):
+        theirs = opp + 1 - 2 * core
+        pos = 10 + t
+        return rcopy(part.at[i, rows(0, theirs), tiles[t]], ra.at[i, 0, :, tiles[t]], rs_send.at[i, pos], rs_recv.at[i, pos], partner)
+
     def rs_a(i):
-        for role in range(4):
+        for role in range(1, 4):
             rs_d2d(i, role).start()
 
     def rs_b(i):
-        rs_d2d(i, 0).wait_recv()
-        rs_add(i, opp, every, ra[i, 0])
-        rs_ring(i, 0).start()
-        rs_ring(i, 1).start()
+        for side, cols in enumerate((lo, hi)):
+            for t in range(n_tiles // 2):
+                rs_first(i, side * (n_tiles // 2) + t).wait_recv()
+            rs_add(i, opp, cols, ra[i, 0, :, cols])
+            rs_ring(i, side).start()
 
     def rs_c(i):
         rs_d2d(i, 1).wait_recv()
@@ -111,8 +120,10 @@
         rs_d2d(i, 3).wait_recv()
         for kind in range(2, 6):
             rs_ring(i, kind).wait_recv()
-        for role in range(4):
+        for role in range(1, 4):
             rs_d2d(i, role).wait_send()
+        for t in range(n_tiles):
+            rs_first(i, t).wait_send()
         for kind in range(6):
             rs_ring(i, kind).wait_send()
         return (part[i, rows(0, me), :] + ra[i, 3]) + (rc[i, 0] + rc[i, 1])
@@ -210,13 +221,10 @@
     rounded(n1, 4, lambda x: rms(x)[0])
     pl.semaphore_wait(barrier, 3)
 
-    col_tile = 512
-
     def product(i, lhs_ref, w_ref):
-        @pl.loop(0, width // col_tile)
-        def _(j):
-            cols = pl.ds(pl.multiple_of(j * col_tile, col_tile), col_tile)
-            part[i, :, cols] = mm(lhs_ref[halves[i % 2], :], w_ref[:, cols], NN)
+        for t in range(n_tiles):
+            part[i, :, tiles[t]] = mm(lhs_ref[halves[i % 2], :], w_ref[:, tiles[t]], NN)
+            rs_first(i, t).start()
 
     def finish(i, slot, fin):
         hb = i % 2
@@ -443,7 +451,7 @@
             vm((2, 2, own, width), F32), vm((2, 2, own, width), F32), vm((2, own, width), F32), vm((2, own, width), F32),
             vm((8, ht, width), F32), vm((8, 4, own, width), F32), vm((8, 2, own, width // 2), F32), vm((8, 2, own, width), F32),
             vm((4, tokens, width), F32),
-            dma((2, 6)), dma((12,)), dma((8, 2)), dma((8,)), dma((8, 10)), dma((8, 10)), dma((8, 9)), dma((8, 9))]
+            dma((2, 6)), dma((12,)), dma((8, 2)), dma((8,)), dma((8, 14)), dma((8, 14)), dma((8, 9)), dma((8, 9))]
         *ends, n1, n2, c_val, e_val, h_val, u_val, a_val, d_val = pl.pallas_call(
             functools.partial(chain_kernel, (n_layers, tp, seq, width, heads, hd)),
             out_shape=(jax.ShapeDtypeStruct((tokens, width), F32),) * 4 + (stack(width), stack(width), stack(width), stack(width),

time: 292 us -> 287 us (0.983)
  Pallas kernels: 291 us -> 285 us
    pallas_call x1, Pallas kernels: 256 us -> 250 us  [local_fn(): pl.pallas_call(functools.partial(chain_kernel, (n_layers, tp, seq, width,...]
where the time goes in v6:
time: 287 us; the launch traced here: 286 us
  Pallas kernels  285 us (99%)
    pallas_call x1, Pallas kernels, local_fn(): pl.pallas_call(functools.partial(chain_kernel, (n_layers, tp, seq, width,...  250 us
    pallas_call x1, Pallas kernels, local_fn(): pl.pallas_call(functools.partial(grad_kernel, (qw, hd)), grid=(n_layers,...  35.2 us

profile of v6, /device:TPU:113, one launch (start us, length us, event | category | flops | bytes accessed | tf_op | source)
XLA Modules:
  0.0 286.1 jit_solution(4610640472031795375)
XLA Ops:
  0.6 250.2 %chain.1 = (f32[256,2048]{1,0:T(8,128)}, f32[256,2048]{1,0:T(8,128)}, f32[256,2048]{1,0:T(8,128)}, f32[256,2048]{1,0:T(8,128)}, bf16[4,256,2048]{2,1,0:T(8,128)(...) custom-call(s32[8]{0:T(128)} %lens.1, ...), custom_call_target="tpu_custom_call" | custom-call | tf_op jit(solution)/shard_map/chain/pallas_call | solution.py:455
  250.9 35.2 %grads.1 = (f32[4,704,2048]{2,1,0:T(8,128)}, f32[4,704,2048]{2,1,0:T(8,128)}, f32[4,256,2048]{2,1,0:T(8,128)}, f32[4,64,2048]{2,1,0:T(8,128)}, f32[4,64,2048]{2,...) custom-call(bf16[4,256,2048]{2,1,0:T(8,128)(2,1)} %get-tuple-element, ...), custom_call_target="tpu_custom_call" | custom-call | flops 8589934592 | bytes 88080384 | tf_op jit(solution)/shard_map/grads/pallas_call | solution.py:477

commit v7 on v6

--- a/solution.py
+++ b/solution.py
@@ -10,6 +10,7 @@
 F32 = jnp.float32
 BF16 = jnp.bfloat16
 EPS = 1e-5
+ORDER = 'AEDPSHBGCI'
 MASK_VALUE = -1e30
 GELU_C = 0.7978845608028654
 GELU_A = 0.044715
@@ -340,29 +341,31 @@
             w = (i - back) % 8
             if i < back:
                 pl.when(later)(lambda: fn(w))
-            elif fn is rs_d:
+            elif fn is rs_d or fn is rs_c:
                 fn(w)
             else:
                 either(fn, w, end)
 
-        for i in range(8):
-            if i < 2:
-                pl.when(later)(lambda: finish((i - 2) % 8, 1 - slot, False))
+        def end_of(i, back):
+            w = (i - back) % 8
+            if i < back:
+                pl.when(later)(lambda: finish(w, 1 - slot, False))
             else:
-                finish(i - 2, slot, end)
-            compute(i)
-            guarded(rs_d, i, 1)
-            guarded(ag_h, i, 3)
-            send(i)
+                finish(w, slot, end)
+
+        def start_up(i):
             if i == 0:
                 @pl.when(step == 0)
                 def _():
                     y_loads[1].wait()
                     rounded(n1, 5, lambda x: rms(x)[0])
-            rs_b(i)
-            guarded(ag_g, i, 2)
-            rs_c(i)
-            guarded(ag_i, i, 3)
+
+        ops = {'E': lambda i: end_of(i, 2), 'A': compute, 'D': lambda i: guarded(rs_d, i, 1), 'H': lambda i: guarded(ag_h, i, 3),
+               'P': send, 'S': start_up, 'B': rs_b, 'G': lambda i: guarded(ag_g, i, 2), 'C': rs_c, 'c': lambda i: guarded(rs_c, i, 1),
+               'I': lambda i: guarded(ag_i, i, 3), 'h': lambda i: guarded(ag_h, i, 2), 'e': lambda i: end_of(i, 1), 'i': lambda i: guarded(ag_i, i, 4)}
+        for i in range(8):
+            for op in ORDER:
+                ops[op](i)
             if i == 1:
                 @pl.when(step == 0)
                 def _():
@@ -384,6 +387,8 @@
                 out_copy(k, hb, src, dst, layer).wait()
 
     last = (n_layers - 1) % 2
+    if 'c' in ORDER:
+        rs_c(7)
     rs_d(7)
     finish(6, last, True)
     ag_h(5, True)

time: 287 us -> 279 us (0.972)
  Pallas kernels: 285 us -> 277 us
    pallas_call x1, Pallas kernels: 250 us -> 242 us  [local_fn(): pl.pallas_call(functools.partial(chain_kernel, (n_layers, tp, seq, width,...]
where the time goes in v7:
time: 279 us; the launch traced here: 278 us
  Pallas kernels  277 us (99%)
    pallas_call x1, Pallas kernels, local_fn(): pl.pallas_call(functools.partial(chain_kernel, (n_layers, tp, seq, width,...  242 us
    pallas_call x1, Pallas kernels, local_fn(): pl.pallas_call(functools.partial(grad_kernel, (qw, hd)), grid=(n_layers,...  35.2 us

profile of v7, /device:TPU:113, one launch (start us, length us, event | category | flops | bytes accessed | tf_op | source)
XLA Modules:
  0.0 277.9 jit_solution(8376320572528234111)
XLA Ops:
  0.6 242.0 %chain.1 = (f32[256,2048]{1,0:T(8,128)}, f32[256,2048]{1,0:T(8,128)}, f32[256,2048]{1,0:T(8,128)}, f32[256,2048]{1,0:T(8,128)}, bf16[4,256,2048]{2,1,0:T(8,128)(...) custom-call(s32[8]{0:T(128)} %lens.1, ...), custom_call_target="tpu_custom_call" | custom-call | tf_op jit(solution)/shard_map/chain/pallas_call | solution.py:460
  242.7 35.2 %grads.1 = (f32[4,704,2048]{2,1,0:T(8,128)}, f32[4,704,2048]{2,1,0:T(8,128)}, f32[4,256,2048]{2,1,0:T(8,128)}, f32[4,64,2048]{2,1,0:T(8,128)}, f32[4,64,2048]{2,...) custom-call(bf16[4,256,2048]{2,1,0:T(8,128)(2,1)} %get-tuple-element, ...), custom_call_target="tpu_custom_call" | custom-call | flops 8589934592 | bytes 88080384 | tf_op jit(solution)/shard_map/grads/pallas_call | solution.py:482

commit v8 on v7

--- a/solution.py
+++ b/solution.py
@@ -341,7 +341,7 @@
             w = (i - back) % 8
             if i < back:
                 pl.when(later)(lambda: fn(w))
-            elif fn is rs_d or fn is rs_c:
+            elif fn is rs_d:
                 fn(w)
             else:
                 either(fn, w, end)
@@ -361,8 +361,8 @@
                     rounded(n1, 5, lambda x: rms(x)[0])
 
         ops = {'E': lambda i: end_of(i, 2), 'A': compute, 'D': lambda i: guarded(rs_d, i, 1), 'H': lambda i: guarded(ag_h, i, 3),
-               'P': send, 'S': start_up, 'B': rs_b, 'G': lambda i: guarded(ag_g, i, 2), 'C': rs_c, 'c': lambda i: guarded(rs_c, i, 1),
-               'I': lambda i: guarded(ag_i, i, 3), 'h': lambda i: guarded(ag_h, i, 2), 'e': lambda i: end_of(i, 1), 'i': lambda i: guarded(ag_i, i, 4)}
+               'P': send, 'S': start_up, 'B': rs_b, 'G': lambda i: guarded(ag_g, i, 2), 'C': rs_c,
+               'I': lambda i: guarded(ag_i, i, 3)}
         for i in range(8):
             for op in ORDER:
                 ops[op](i)
@@ -387,8 +387,6 @@
                 out_copy(k, hb, src, dst, layer).wait()
 
     last = (n_layers - 1) % 2
-    if 'c' in ORDER:
-        rs_c(7)
     rs_d(7)
     finish(6, last, True)
     ag_h(5, True)
@@ -468,7 +466,7 @@
             name='chain',
         )(seq_lens, *acts, *weights)
 
-        col_tile = 512
+        col_tile = 1024
 
         def wide():
             return pl.BlockSpec((1, tokens, col_tile), lambda layer, j: (layer, 0, j))

time: 279 us -> 277 us (level)
  no operation moved by 1% of the time
where the time goes in v8:
time: 277 us
  Pallas kernels  276 us (100%)
    pallas_call x1, Pallas kernels, local_fn(): pl.pallas_call(functools.partial(chain_kernel, (n_layers, tp, seq, width,...  242 us
    pallas_call x1, Pallas kernels, local_fn(): pl.pallas_call(functools.partial(grad_kernel, (qw, hd)), grid=(n_layers,...  34.3 us

profile of v8, /device:TPU:113, one launch (start us, length us, event | category | flops | bytes accessed | tf_op | source)
XLA Modules:
  0.0 277.1 jit_solution(4730735112798113129)
XLA Ops:
  0.6 242.1 %chain.1 = (f32[256,2048]{1,0:T(8,128)}, f32[256,2048]{1,0:T(8,128)}, f32[256,2048]{1,0:T(8,128)}, f32[256,2048]{1,0:T(8,128)}, bf16[4,256,2048]{2,1,0:T(8,128)(...) custom-call(s32[8]{0:T(128)} %lens.1, ...), custom_call_target="tpu_custom_call" | custom-call | tf_op jit(solution)/shard_map/chain/pallas_call | solution.py:458
  242.7 34.3 %grads.1 = (f32[4,704,2048]{2,1,0:T(8,128)}, f32[4,704,2048]{2,1,0:T(8,128)}, f32[4,256,2048]{2,1,0:T(8,128)}, f32[4,64,2048]{2,1,0:T(8,128)}, f32[4,64,2048]{2,...) custom-call(bf16[4,256,2048]{2,1,0:T(8,128)(2,1)} %get-tuple-element, ...), custom_call_target="tpu_custom_call" | custom-call | flops 8589934592 | bytes 88080384 | tf_op jit(solution)/shard_map/grads/pallas_call | solution.py:480
